TPU v7x, 128 devices: a whole 4x4x4 slice. The times are simulated.
128 devices in a mesh: row: 16 (over x, y), col: 8 (over z, core).
Axes of the slice: x: 4, y: 4, z: 4, core: 2. Of those that a mesh axis runs over, the one named last changes fastest.
Arguments:
- fast_pos: float32 [3, 4096], P(None, ('row', 'col')), may hold values from 0 to 1
- fast_vel: float32 [3, 4096], P(None, ('row', 'col')), may hold values from -5 to 5
- fast_charge: float32 [4096], replicated, may hold values from -4 to 4
- fast_owner: int32 [4096], replicated, may hold values from 0 to 4095, as said below
- exclusions: int32 [4096, 4], replicated, may hold values from 0 to 4095, as said below
- slow_pos: float32 [3, 64, 64, 128], P(None, 'row', 'col'), may hold values from 0 to 1
- slow_vel: float32 [3, 64, 64, 128], P(None, 'row', 'col'), may hold values from -5 to 5
- slow_charge: float32 [64, 64, 128], P('row', 'col'), may hold values from -4 to 4
- neighbours: int32 [64, 64, 5], P('row', 'col'), may hold values from 0 to 24, all different within a row
Outputs:
- fast_pos_out: float32 [3, 4096], P(None, ('row', 'col'))
- fast_vel_out: float32 [3, 4096], P(None, ('row', 'col'))
- slow_pos_out: float32 [3, 64, 64, 128], P(None, 'row', 'col')
- slow_vel_out: float32 [3, 64, 64, 128], P(None, 'row', 'col')
Inputs may be any that keep to these rules, and one draw needn't show every extreme that they name: `fast_owner`: atoms a and b with a % (256) == b % (256) share an owner. `exclusions`: the partners of atom a are atoms b != a with b % (256) == a % 256; a partner may repeat. `neighbours`: the entries of one cell are distinct.
All inputs are finite; a program needn't handle non-finite values.
Results may differ from a plain program's by a relative error of at most 0.0003.
Values sent between devices are 32-bit elements; how exact they have to be, the bound alone decides.
A program may use at most 64 MiB of HBM per device.

v0:
```python
import jax
import jax.numpy as jnp
from jax import lax
from jax.experimental import pallas as pl
from jax.experimental.pallas import tpu as pltpu
from jax.sharding import PartitionSpec as P

MESH = pl.DeviceIdType.MESH
FAST = 4096
CELL = 128
NBR = 5
INNER = 4
ROWS, COLS = 16, 8
MOL = FAST // ROWS
PIECE = MOL // COLS
CR, CC = 4, 8
CELLS = CR * CC
TOTAL_COLS = 64

fast_coupling = 1.0
slow_coupling = 0.1
outer_dt = 0.2
half_outer = 0.5 * outer_dt
inner_dt = outer_dt / INNER

SIDES = [(a, b) for a in (-1, 0, 1) for b in (-1, 0, 1) if (a, b) != (0, 0)]


def column(row):
    return jnp.transpose(jnp.broadcast_to(row, (128, 128)))


def kernel(
    own_ref, charge_ref, owner_ref, excl_ref, spos_ref, svel_ref, scharge_ref, nbr_ref,
    fpos_out, fvel_out, spos_out, svel_out,
    zrecv, gath, mat, esend, erecv, zsend2, zrecv2, acol, facc, halo_0, halo_1, scol, sacc, sforce, table, corner, barred,
    z_send, z_recv, g_send, g_recv, e_send, e_recv, y_send, y_recv, h_send, h_recv,
):
    row = lax.axis_index("row")
    col = lax.axis_index("col")
    halos = (halo_0, halo_1)
    px, py = lax.div(row, 4), lax.rem(row, 4)

    def turn(u):
        return u + lax.div(u, 2) * (5 - 2 * u)

    def peer(t):
        if isinstance(t, int):
            dx, dy = (0, 1, 3, 2)[t // 4], (0, 1, 3, 2)[t % 4]
        else:
            dx, dy = turn(lax.div(t, 4)), turn(lax.rem(t, 4))
        return lax.rem(px + dx, 4) * 4 + lax.rem(py + dy, 4)

    def line(t):
        return lax.rem(col + t, COLS)

    def side(a, b):
        return lax.rem(row + (a + ROWS), ROWS), lax.rem(col + (b + COLS), COLS)

    def remote(src, dst, send, recv, to):
        return pltpu.make_async_remote_copy(
            src_ref=src, dst_ref=dst, send_sem=send, recv_sem=recv, device_id=to, device_id_type=MESH
        )

    barrier = pltpu.get_barrier_semaphore()
    partners = [(peer(t), col) for t in range(1, ROWS)] + [(row, line(t)) for t in range(1, COLS)]
    partners += [side(a, b) for a, b in SIDES if a and b]
    for to in partners:
        pl.semaphore_signal(barrier, inc=1, device_id=to, device_id_type=MESH)

    def fill_halo(buf, pos):
        for r in range(CR):
            for comp in range(4):
                v = scharge_ref[r * CC : r * CC + CC, :] if comp == 3 else pos[comp, r * CC : r * CC + CC, :]
                for c in range(CC):
                    halos[buf][2 + r, 2 + c, comp : comp + 1, :] = v[c : c + 1, :]

    def halo_copy(buf, d):
        a, b = SIDES[d]
        rs, rd, rn = {-1: (2, 6, 2), 0: (2, 2, 4), 1: (4, 0, 2)}[a]
        cs, cd, cn = {-1: (2, 10, 2), 0: (2, 2, 8), 1: (8, 0, 2)}[b]
        return remote(
            halos[buf].at[rs : rs + rn, cs : cs + cn],
            halos[buf].at[rd : rd + rn, cd : cd + cn],
            h_send.at[buf, d],
            h_recv.at[buf, d],
            side(a, b),
        )

    def slow_columns(pos, c0, c1):
        def body(c, carry):
            for comp in range(3):
                scol[c, comp] = column(pos[comp, pl.ds(c, 1), :])
            return carry

        lax.fori_loop(c0, c1, body, 0)

    def slow_pairs(buf, c0, c1):
        def body(c, carry):
            r, k = lax.div(c, CC), lax.rem(c, CC)
            others = []
            for slot in range(NBR):
                o = nbr_ref[c, slot]
                dr = lax.div(o, 5)
                dc = o - 5 * dr
                tile = halos[buf][r + dr, k + dc]
                others.append(
                    (
                        jnp.broadcast_to(tile[0:1] + (dr - 2).astype(jnp.float32), (8, 128)),
                        jnp.broadcast_to(tile[1:2] + (dc - 2).astype(jnp.float32), (8, 128)),
                        jnp.broadcast_to(tile[2:3], (8, 128)),
                        jnp.broadcast_to(tile[3:4], (8, 128)),
                    )
                )
            for i in range(16):
                x = scol[c, 0, 8 * i : 8 * i + 8, :]
                y = scol[c, 1, 8 * i : 8 * i + 8, :]
                z = scol[c, 2, 8 * i : 8 * i + 8, :]
                fx = fy = fz = None
                for ox, oy, oz, oq in others:
                    dx, dy, dz = x - ox, y - oy, z - oz
                    s = (dx * dx + dy * dy) + (dz * dz + 0.5)
                    inv = lax.rsqrt(s)
                    w = (inv * inv) * (inv * oq)
                    if fx is None:
                        fx, fy, fz = w * dx, w * dy, w * dz
                    else:
                        fx, fy, fz = fx + w * dx, fy + w * dy, fz + w * dz
                sacc[c, 0, 8 * i : 8 * i + 8, :] = fx
                sacc[c, 1, 8 * i : 8 * i + 8, :] = fy
                sacc[c, 2, 8 * i : 8 * i + 8, :] = fz
            return carry

        lax.fori_loop(c0, c1, body, 0)

    def slow_sums(c0, c1):
        def body(c, carry):
            for comp in range(3):
                sforce[comp, pl.ds(c, 1), :] = jnp.sum(jnp.transpose(sacc[c, comp]), axis=0, keepdims=True)
            return carry

        lax.fori_loop(c0, c1, body, 0)

    def fill_table(pos):
        owner = owner_ref[...]
        gr = lax.shift_right_logical(owner, 6) - row * CR
        gc = (owner & 63) - col * CC
        inside = (gr >= 0) & (gr < CR) & (gc >= 0) & (gc < CC)
        local = jnp.where(inside, gr * CC + gc, -1)
        ids = lax.broadcasted_iota(jnp.int32, (CELLS, MOL), 0)
        pick = jnp.where(jnp.broadcast_to(local, (CELLS, MOL)) == ids, 1.0, 0.0).astype(jnp.float32)
        for comp in range(4):
            data = scharge_ref[...] if comp == 3 else pos[comp]
            table[comp * CELL : (comp + 1) * CELL, :] = jnp.dot(
                jnp.transpose(data), pick, precision=lax.Precision.HIGHEST, preferred_element_type=jnp.float32
            )

    def env_start(buf):
        mx, my, mz = mat[0], mat[1], mat[2]

        def body(jb, carry):
            fx, fy, fz = carry
            for k in range(4):
                j = jb * 4 + k
                ox, oy, oz, oq = (
                    jnp.broadcast_to(table[pl.ds(comp * CELL + j, 1), :], (ROWS, MOL)) for comp in range(4)
                )
                dx, dy, dz = mx - ox, my - oy, mz - oz
                s = (dx * dx + dy * dy) + (dz * dz + 0.5)
                inv = lax.rsqrt(s)
                w = (inv * inv) * (inv * oq)
                fx, fy, fz = fx + w * dx, fy + w * dy, fz + w * dz
            return fx, fy, fz

        zero = jnp.zeros((ROWS, MOL), jnp.float32)
        force = lax.fori_loop(0, CELL // 4, body, (zero, zero, zero))
        for r in range(ROWS):
            for comp in range(3):
                esend[buf, r, comp : comp + 1, :] = force[comp][r : r + 1, :]
            esend[buf, r, 3:4, :] = jnp.zeros((1, MOL), jnp.float32)
        for t in range(ROWS - 1, 0, -1):
            to = peer(t)
            remote(esend.at[buf, to], erecv.at[buf, row], e_send.at[buf], e_recv.at[buf], (to, col)).start()
        erecv[buf, row] = esend[buf, row]

    def env_middle(buf):
        whole = erecv.at[buf, 0 : ROWS - 1]
        remote(whole, whole, e_send.at[buf], e_recv.at[buf], (row, line(1))).wait_recv()
        total = erecv[buf, 0]
        for r in range(1, ROWS):
            total = total + erecv[buf, r]
        zsend2[buf] = total
        for t in range(COLS - 1, 0, -1):
            remote(zsend2.at[buf], zrecv2.at[buf, col], y_send.at[buf], y_recv.at[buf], (row, line(t))).start()
        zrecv2[buf, col] = total

    def env_end(buf):
        whole = zrecv2.at[buf, 0 : COLS - 1]
        remote(whole, whole, y_send.at[buf], y_recv.at[buf], (row, line(1))).wait_recv()
        total = zrecv2[buf, 0]
        for c in range(1, COLS):
            total = total + zrecv2[buf, c]
        return (slow_coupling * own_charge) * total

    def gather_start(g, pos):
        gath[g, row] = pos
        for t in range(ROWS - 1, 0, -1):
            remote(gath.at[g, row], gath.at[g, row], g_send.at[g], g_recv.at[g, row], (peer(t), col)).start()
        for comp in range(3):
            line_ = pos[comp : comp + 1, :]
            mat[comp, pl.ds(row, 1), :] = line_
            if comp < 2:
                line_ = line_ + corner[comp : comp + 1, :]
            for h in range(2):
                acol[comp, 128 * h : 128 * h + 128, :] = column(line_[:, 128 * h : 128 * h + 128])
        facc[...] = jnp.zeros_like(facc)

    def arrive(g, t):
        r = peer(t)
        slot = gath.at[g, r]
        remote(slot, slot, g_send.at[g], g_recv.at[g, r], (r, col)).wait_recv()
        for comp in range(3):
            mat[comp, pl.ds(r, 1), :] = gath[g, r, comp : comp + 1, :]

    def fast_row(g, t):
        r = peer(t)
        tile = gath[g, r]
        lines = (
            tile[0:1] + corner[0:1, :],
            tile[1:2] + corner[1:2, :],
            tile[2:3],
            charge_ref[pl.ds(r, 1), :],
        )
        halves = [[jnp.broadcast_to(v[:, 128 * h : 128 * h + 128], (8, 128)) for v in lines] for h in range(2)]
        for i in range(MOL // 8):
            x = acol[0, 8 * i : 8 * i + 8, :]
            y = acol[1, 8 * i : 8 * i + 8, :]
            z = acol[2, 8 * i : 8 * i + 8, :]
            fx = facc[0, 8 * i : 8 * i + 8, :]
            fy = facc[1, 8 * i : 8 * i + 8, :]
            fz = facc[2, 8 * i : 8 * i + 8, :]
            for ox, oy, oz, oq in halves:
                dx, dy, dz = x - ox, y - oy, z - oz
                s = (dx * dx + dy * dy) + (dz * dz + 1.0)
                inv = lax.rsqrt(s)
                w = (inv * inv) * (inv * oq)
                fx, fy, fz = fx + w * dx, fy + w * dy, fz + w * dz
            facc[0, 8 * i : 8 * i + 8, :] = fx
            facc[1, 8 * i : 8 * i + 8, :] = fy
            facc[2, 8 * i : 8 * i + 8, :] = fz

    def fast_rows(g, t0, t1, waiting):
        def body(t, carry):
            if waiting:
                arrive(g, t)
            fast_row(g, t)
            return carry

        lax.fori_loop(t0, t1, body, 0)

    def arrivals(g, t0, t1):
        def body(t, carry):
            arrive(g, t)
            return carry

        lax.fori_loop(t0, t1, body, 0)

    def fast_end(pos):
        d = [jnp.broadcast_to(pos[comp : comp + 1, :], (ROWS, MOL)) - mat[comp] for comp in range(3)]
        s = (d[0] * d[0] + d[1] * d[1]) + (d[2] * d[2] + 1.0)
        inv = lax.rsqrt(s)
        w = (inv * inv) * (inv * barred[...])
        out = []
        for comp in range(3):
            parts = [
                jnp.sum(jnp.transpose(facc[comp, 128 * h : 128 * h + 128, :]), axis=0, keepdims=True) for h in range(2)
            ]
            total = jnp.concatenate(parts, axis=1)
            out.append(total - jnp.sum(w * d[comp], axis=0, keepdims=True))
        out.append(jnp.zeros((1, MOL), jnp.float32))
        return (fast_coupling * own_charge) * jnp.concatenate(out, axis=0)

    fill_halo(0, spos_ref)
    pl.semaphore_wait(barrier, len(partners))
    for t in range(COLS - 1, 0, -1):
        remote(own_ref, zrecv.at[col], z_send, z_recv, (row, line(t))).start()
    for d in range(8):
        halo_copy(0, d).start()
    zrecv[col] = own_ref[...]
    own_charge = charge_ref[pl.ds(row, 1), :]
    owner = owner_ref[...]
    corner[0:1, :] = lax.shift_right_logical(owner, 6).astype(jnp.float32)
    corner[1:2, :] = (owner & 63).astype(jnp.float32)
    index = lax.broadcasted_iota(jnp.int32, (ROWS, MOL), 0) * MOL + lax.broadcasted_iota(jnp.int32, (ROWS, MOL), 1)
    hit = jnp.broadcast_to(excl_ref[0:1, :], (ROWS, MOL)) == index
    for e in range(1, 4):
        hit = hit | (jnp.broadcast_to(excl_ref[e : e + 1, :], (ROWS, MOL)) == index)
    barred[...] = jnp.where(hit, charge_ref[...], 0.0)
    fill_table(spos_ref)
    slow_columns(spos_ref, 0, CELLS)

    whole = zrecv.at[0 : COLS - 1]
    remote(whole, whole, z_send, z_recv, (row, line(1))).wait_recv()
    both = zrecv[0]
    for c in range(1, COLS):
        both = both + zrecv[c]
    pos, vel = both[0:4], both[4:8]

    gather_start(0, pos)
    for d in range(8):
        halo_copy(0, d).wait_recv()
    slow_pairs(0, 0, 12)
    arrivals(0, 1, ROWS)
    env_start(0)
    fast_rows(0, 0, ROWS, False)
    force = fast_end(pos)
    slow_pairs(0, 12, 18)
    env_middle(0)
    slow_pairs(0, 18, 30)
    vel = vel + half_outer * env_end(0)
    for g in range(1, INNER + 1):
        vel = vel + (0.5 * inner_dt) * force
        pos = pos + inner_dt * vel
        gather_start(g, pos)
        if g == 1:
            slow_pairs(0, 30, 32)
            slow_sums(0, CELLS)
            for comp in range(3):
                v = svel_ref[comp] + half_outer * ((slow_coupling * scharge_ref[...]) * sforce[comp])
                svel_out[comp] = v
                spos_out[comp] = spos_ref[comp] + outer_dt * v
            fill_halo(1, spos_out)
            for d in range(8):
                halo_copy(1, d).start()
        elif g == 2:
            slow_columns(spos_out, 0, CELLS)
            fill_table(spos_out)
        elif g == 3:
            for d in range(8):
                halo_copy(1, d).wait_recv()
            slow_pairs(1, 0, 8)
        else:
            slow_pairs(1, 8, 16)
        if g < INNER:
            fast_rows(g, 0, 1, False)
            fast_rows(g, 1, ROWS, True)
            force = fast_end(pos)
            vel = vel + (0.5 * inner_dt) * force
        else:
            fast_rows(g, 0, 1, False)
            fast_rows(g, 1, 12, True)
            arrivals(g, 12, ROWS)
            env_start(1)
            fast_rows(g, 12, ROWS, False)
            force = fast_end(pos)
            vel = vel + (0.5 * inner_dt) * force
    slow_pairs(1, 16, 26)
    env_middle(1)
    slow_pairs(1, 26, 32)
    slow_sums(0, CELLS)
    for comp in range(3):
        svel_out[comp] = svel_out[comp] + half_outer * ((slow_coupling * scharge_ref[...]) * sforce[comp])
    vel = vel + half_outer * env_end(1)
    back = lax.rem(MOL - col * PIECE, MOL)
    for value, out in ((pos, fpos_out), (vel, fvel_out)):
        out[...] = pltpu.roll(jnp.concatenate([value, value], axis=0), back, 1)[0:3, 0:PIECE]

    whole = zrecv.at[0 : COLS - 1]
    remote(whole, whole, z_send, z_recv, (row, line(1))).wait_send()
    for buf in range(2):
        for d in range(8):
            halo_copy(buf, d).wait_send()
        whole = erecv.at[buf, 0 : ROWS - 1]
        remote(whole, whole, e_send.at[buf], e_recv.at[buf], (row, line(1))).wait_send()
        whole = zrecv2.at[buf, 0 : COLS - 1]
        remote(whole, whole, y_send.at[buf], y_recv.at[buf], (row, line(1))).wait_send()
    for g in range(INNER + 1):
        whole = gath.at[g, 0 : ROWS - 1]
        remote(whole, whole, g_send.at[g], g_recv.at[g, 0], (row, line(1))).wait_send()


def per_device(fast_pos, fast_vel, fast_charge, fast_owner, exclusions, slow_pos, slow_vel, slow_charge, neighbours):
    row, col = lax.axis_index("row"), lax.axis_index("col")
    own = jnp.concatenate([jnp.pad(fast_pos, ((0, 1), (0, 0))), jnp.pad(fast_vel, ((0, 1), (0, 0)))], axis=0)
    own = lax.dynamic_update_slice(jnp.zeros((8, MOL), jnp.float32), own, (0, col * PIECE))
    charge = fast_charge.reshape(ROWS, MOL)
    owner = fast_owner[:MOL].reshape(1, MOL)
    excl = lax.dynamic_slice(exclusions, (row * MOL, 0), (MOL, 4)).T
    f32 = jnp.float32
    vmem = pl.BlockSpec(memory_space=pltpu.VMEM)
    dma = pltpu.SemaphoreType.DMA
    outs = pl.pallas_call(
        kernel,
        out_shape=(
            jax.ShapeDtypeStruct((3, PIECE), f32),
            jax.ShapeDtypeStruct((3, PIECE), f32),
            jax.ShapeDtypeStruct((3, CELLS, CELL), f32),
            jax.ShapeDtypeStruct((3, CELLS, CELL), f32),
        ),
        in_specs=[vmem] * 7 + [pl.BlockSpec(memory_space=pltpu.SMEM)],
        out_specs=(vmem,) * 4,
        scratch_shapes=[
            pltpu.VMEM((COLS, 8, MOL), f32),
            pltpu.VMEM((INNER + 1, ROWS, 4, MOL), f32),
            pltpu.VMEM((3, ROWS, MOL), f32),
            pltpu.VMEM((2, ROWS, 4, MOL), f32),
            pltpu.VMEM((2, ROWS, 4, MOL), f32),
            pltpu.VMEM((2, 4, MOL), f32),
            pltpu.VMEM((2, COLS, 4, MOL), f32),
            pltpu.VMEM((3, MOL, 128), f32),
            pltpu.VMEM((3, MOL, 128), f32),
            pltpu.VMEM((CR + 4, CC + 4, 4, CELL), f32),
            pltpu.VMEM((CR + 4, CC + 4, 4, CELL), f32),
            pltpu.VMEM((CELLS, 3, CELL, CELL), f32),
            pltpu.VMEM((CELLS, 3, CELL, CELL), f32),
            pltpu.VMEM((3, CELLS, CELL), f32),
            pltpu.VMEM((4 * CELL, MOL), f32),
            pltpu.VMEM((2, MOL), f32),
            pltpu.VMEM((ROWS, MOL), f32),
            dma,
            dma,
            dma((INNER + 1,)),
            dma((INNER + 1, ROWS)),
            dma((2,)),
            dma((2,)),
            dma((2,)),
            dma((2,)),
            dma((2, 8)),
            dma((2, 8)),
        ],
        compiler_params=pltpu.CompilerParams(
            collective_id=0, has_side_effects=True, vmem_limit_bytes=40 * 1024 * 1024
        ),
    )(
        own,
        charge,
        owner,
        excl,
        slow_pos.reshape(3, CELLS, CELL),
        slow_vel.reshape(3, CELLS, CELL),
        slow_charge.reshape(CELLS, CELL),
        neighbours.reshape(CELLS, NBR),
    )
    fpos, fvel, spos, svel = outs
    return fpos, fvel, spos.reshape(3, CR, CC, CELL), svel.reshape(3, CR, CC, CELL)


def solution(mesh):
    specs = (
        P(None, ("row", "col")),
        P(None, ("row", "col")),
        P(),
        P(),
        P(),
        P(None, "row", "col", None),
        P(None, "row", "col", None),
        P("row", "col", None),
        P("row", "col", None),
    )
    return jax.shard_map(
        per_device,
        mesh=mesh,
        in_specs=specs,
        out_specs=(specs[0], specs[1], specs[5], specs[6]),
        check_vma=False,
    )
```

profile of v0, /device:TPU:0, one launch (start us, length us, event | category | flops | bytes accessed | tf_op | source)
XLA Modules:
  0.0 76.4 jit_solution(2836968693851587901)
XLA Ops:
  0.6 0.0 copy-start
  0.6 0.0 copy-start.5
  0.7 0.0 copy-start.4
  0.7 0.0 copy-start.3
  0.7 0.0 copy-start.2
  0.7 0.7 slice.3
  1.4 0.0 copy-start.1
  1.4 0.0 copy-done
  1.5 0.0 copy-done.5
  1.5 0.7 select_maximum_fusion
  2.2 0.3 dynamic_update_slice.3.own_ref
  2.4 0.0 copy-done.4
  2.5 0.8 %copy.13 = s32[4,8,5]{2,1,0:T(8,128)S(1)} copy(s32[4,8,5]{1,0,2:T(4,128)} %param.17) | data formatting | bytes 1280 | tf_op args[8]
  3.3 0.0 copy-done.3
  3.3 0.0 copy-done.2
  3.3 0.0 copy-done.1
  3.3 70.7 %shard_map.120 = (f32[3,32]{1,0:T(4,128)S(1)}, f32[3,32]{1,0:T(4,128)S(1)}, f32[3,32,128]{2,1,0:T(8,128)S(1)}, f32[3,32,128]{2,1,0:T(8,128)S(1)}) custom-call(f32[8,256]{1,0:T(8,128)S(1)} %dynamic_update_slice.3.own_ref, f32[16,256]{1,0:T(8,128)S(1)} %reshape.32.charge_ref, s32[1,256]{1,0:T(1,128)S(1)} %bitcast.15, ...), custom_call_target="tpu_custom_call" | custom-call | tf_op jit(solution)/shard_map/pallas_call | solution.py:392
  74.0 0.6 copy.19
  74.6 0.6 copy.20
  75.1 0.6 copy.21
  75.8 0.6 copy.22
  (3 shorter events, 0.0 us)
Async XLA Ops:
  0.6 0.8 %copy-start = (s32[4096,4]{0,1:T(4,128)S(1)}, s32[4096,4]{0,1:T(4,128)}, u32[]{:S(2)}) copy-start(s32[4096,4]{0,1:T(4,128)} %param.13) | copy-start | bytes 196612
  0.6 0.8 %copy-start.5 = (f32[3,32]{1,0:T(4,128)S(1)}, f32[3,32]{1,0:T(4,128)}, u32[]{:S(2)}) copy-start(f32[3,32]{1,0:T(4,128)} %param.10) | copy-start | bytes 1156
  0.7 1.8 %copy-start.4 = (f32[4096]{0:T(1024)S(1)}, f32[4096]{0:T(1024)}, u32[]{:S(2)}) copy-start(f32[4096]{0:T(1024)} %param.11) | copy-start | bytes 49156
  0.7 2.6 %copy-start.3 = (f32[4,8,128]{2,1,0:T(8,128)S(1)}, f32[4,8,128]{2,1,0:T(8,128)}, u32[]{:S(2)}) copy-start(f32[4,8,128]{2,1,0:T(8,128)} %param.16) | copy-start | bytes 49156
  0.7 2.6 %copy-start.2 = (f32[3,4,8,128]{3,2,1,0:T(8,128)S(1)}, f32[3,4,8,128]{3,2,1,0:T(8,128)}, u32[]{:S(2)}) copy-start(f32[3,4,8,128]{3,2,1,0:T(8,128)} %param.15) | copy-start | bytes 147460
  1.4 1.8 %copy-start.1 = (f32[3,4,8,128]{3,2,1,0:T(8,128)S(1)}, f32[3,4,8,128]{3,2,1,0:T(8,128)}, u32[]{:S(2)}) copy-start(f32[3,4,8,128]{3,2,1,0:T(8,128)} %param.14) | copy-start | bytes 147460
where the time goes:
time: 76.6 us; the launch traced here: 76.4 us
  Pallas kernels  70.7 us (92%)
  local copies, waits for them, and re-layouts  4.27 us (6%)
    pallas_call x1, Pallas kernels, per_device(): pl.pallas_call(kernel, out_shape=(jax.ShapeDtypeStruct((3, PIECE), f32),...  70.7 us
    unnamed x17, local copies, waits for them, and re-layouts  3.27 us

commit v1 on v0

--- a/solution.py
+++ b/solution.py
@@ -31,10 +31,10 @@
 
 
 def kernel(
-    own_ref, charge_ref, owner_ref, excl_ref, spos_ref, svel_ref, scharge_ref, nbr_ref,
+    fpos_ref, fvel_ref, charge_ref, owner_ref, excl_ref, spos_ref, svel_ref, scharge_ref, nbr_ref,
     fpos_out, fvel_out, spos_out, svel_out,
-    zrecv, gath, mat, esend, erecv, zsend2, zrecv2, acol, facc, halo_0, halo_1, scol, sacc, sforce, table, corner, barred,
-    z_send, z_recv, g_send, g_recv, e_send, e_recv, y_send, y_recv, h_send, h_recv,
+    zrecv, gath, mat, esend, erecv, zsend2, zrecv2, acol, facc, halo_0, halo_1, scol_0, scol_1, sacc_0, sacc_1, sforce, table, zown, dsend, drecv, corner, barred,
+    z_send, z_recv, g_send, g_recv, e_send, e_recv, y_send, y_recv, h_send, h_recv, d_send, d_recv,
 ):
     row = lax.axis_index("row")
     col = lax.axis_index("col")
@@ -87,62 +87,74 @@
             side(a, b),
         )
 
-    def slow_columns(pos, c0, c1):
-        def body(c, carry):
-            for comp in range(3):
-                scol[c, comp] = column(pos[comp, pl.ds(c, 1), :])
+    scols, saccs = (scol_0, scol_1), (sacc_0, sacc_1)
+
+    def slow_columns(pos, c, into):
+        for comp in range(3):
+            into[comp] = column(pos[comp, pl.ds(c, 1), :])
+
+    def slow_sums(c, acc):
+        for comp in range(3):
+            sforce[comp, pl.ds(c, 1), :] = jnp.sum(jnp.transpose(acc[comp]), axis=0, keepdims=True)
+
+    def slow_cell(halo, c, scol, sacc):
+        r, k = lax.div(c, CC), lax.rem(c, CC)
+        others = []
+        for slot in range(NBR):
+            o = nbr_ref[slot, r, k]
+            dr = lax.div(o, 5)
+            dc = o - 5 * dr
+            tile = halo[r + dr, k + dc]
+            others.append(
+                (
+                    jnp.broadcast_to(tile[0:1] + (dr - 2).astype(jnp.float32), (8, 128)),
+                    jnp.broadcast_to(tile[1:2] + (dc - 2).astype(jnp.float32), (8, 128)),
+                    jnp.broadcast_to(tile[2:3], (8, 128)),
+                    jnp.broadcast_to(tile[3:4], (8, 128)),
+                )
+            )
+        for i in range(16):
+            x = scol[0, 8 * i : 8 * i + 8, :]
+            y = scol[1, 8 * i : 8 * i + 8, :]
+            z = scol[2, 8 * i : 8 * i + 8, :]
+            fx = fy = fz = None
+            for ox, oy, oz, oq in others:
+                dx, dy, dz = x - ox, y - oy, z - oz
+                s = (dx * dx + dy * dy) + (dz * dz + 0.5)
+                inv = lax.rsqrt(s)
+                w = (inv * inv) * (inv * oq)
+                if fx is None:
+                    fx, fy, fz = w * dx, w * dy, w * dz
+                else:
+                    fx, fy, fz = fx + w * dx, fy + w * dy, fz + w * dz
+            sacc[0, 8 * i : 8 * i + 8, :] = fx
+            sacc[1, 8 * i : 8 * i + 8, :] = fy
+            sacc[2, 8 * i : 8 * i + 8, :] = fz
+
+    def slow_start(pos):
+        slow_columns(pos, 0, scol_0)
+        sacc_1[...] = jnp.zeros_like(sacc_1)
+
+    def slow_pairs(buf, c0, c1):
+        pos = spos_out if buf else spos_ref
+
+        def body(p, carry):
+            c = 2 * p
+            slow_cell(halos[buf], c, scol_0, sacc_0)
+            slow_sums(lax.max(c - 1, 0), sacc_1)
+            slow_columns(pos, c + 1, scol_1)
+            slow_cell(halos[buf], c + 1, scol_1, sacc_1)
+            slow_sums(c, sacc_0)
+            slow_columns(pos, lax.min(c + 2, CELLS - 1), scol_0)
             return carry
 
-        lax.fori_loop(c0, c1, body, 0)
-
-    def slow_pairs(buf, c0, c1):
-        def body(c, carry):
-            r, k = lax.div(c, CC), lax.rem(c, CC)
-            others = []
-            for slot in range(NBR):
-                o = nbr_ref[c, slot]
-                dr = lax.div(o, 5)
-                dc = o - 5 * dr
-                tile = halos[buf][r + dr, k + dc]
-                others.append(
-                    (
-                        jnp.broadcast_to(tile[0:1] + (dr - 2).astype(jnp.float32), (8, 128)),
-                        jnp.broadcast_to(tile[1:2] + (dc - 2).astype(jnp.float32), (8, 128)),
-                        jnp.broadcast_to(tile[2:3], (8, 128)),
-                        jnp.broadcast_to(tile[3:4], (8, 128)),
-                    )
-                )
-            for i in range(16):
-                x = scol[c, 0, 8 * i : 8 * i + 8, :]
-                y = scol[c, 1, 8 * i : 8 * i + 8, :]
-                z = scol[c, 2, 8 * i : 8 * i + 8, :]
-                fx = fy = fz = None
-                for ox, oy, oz, oq in others:
-                    dx, dy, dz = x - ox, y - oy, z - oz
-                    s = (dx * dx + dy * dy) + (dz * dz + 0.5)
-                    inv = lax.rsqrt(s)
-                    w = (inv * inv) * (inv * oq)
-                    if fx is None:
-                        fx, fy, fz = w * dx, w * dy, w * dz
-                    else:
-                        fx, fy, fz = fx + w * dx, fy + w * dy, fz + w * dz
-                sacc[c, 0, 8 * i : 8 * i + 8, :] = fx
-                sacc[c, 1, 8 * i : 8 * i + 8, :] = fy
-                sacc[c, 2, 8 * i : 8 * i + 8, :] = fz
-            return carry
-
-        lax.fori_loop(c0, c1, body, 0)
-
-    def slow_sums(c0, c1):
-        def body(c, carry):
-            for comp in range(3):
-                sforce[comp, pl.ds(c, 1), :] = jnp.sum(jnp.transpose(sacc[c, comp]), axis=0, keepdims=True)
-            return carry
-
-        lax.fori_loop(c0, c1, body, 0)
+        lax.fori_loop(c0 // 2, c1 // 2, body, 0)
+
+    def slow_end():
+        slow_sums(CELLS - 1, sacc_1)
 
     def fill_table(pos):
-        owner = owner_ref[...]
+        owner = owner_ref[0:1, :]
         gr = lax.shift_right_logical(owner, 6) - row * CR
         gc = (owner & 63) - col * CC
         inside = (gr >= 0) & (gr < CR) & (gc >= 0) & (gc < CC)
@@ -155,7 +167,7 @@
                 jnp.transpose(data), pick, precision=lax.Precision.HIGHEST, preferred_element_type=jnp.float32
             )
 
-    def env_start(buf):
+    def env_partial():
         mx, my, mz = mat[0], mat[1], mat[2]
 
         def body(jb, carry):
@@ -173,7 +185,10 @@
             return fx, fy, fz
 
         zero = jnp.zeros((ROWS, MOL), jnp.float32)
-        force = lax.fori_loop(0, CELL // 4, body, (zero, zero, zero))
+        return lax.fori_loop(0, CELL // 4, body, (zero, zero, zero))
+
+    def env_rows(buf):
+        force = env_partial()
         for r in range(ROWS):
             for comp in range(3):
                 esend[buf, r, comp : comp + 1, :] = force[comp][r : r + 1, :]
@@ -182,6 +197,32 @@
             to = peer(t)
             remote(esend.at[buf, to], erecv.at[buf, row], e_send.at[buf], e_recv.at[buf], (to, col)).start()
         erecv[buf, row] = esend[buf, row]
+
+    def env_direct():
+        force = env_partial()
+        lane = lax.broadcasted_iota(jnp.int32, (ROWS, 128), 1)
+        for c in range(COLS):
+            h, j = c // 4, c % 4
+            line_ = jnp.zeros((ROWS, 128), jnp.float32)
+            for comp in range(3):
+                part = force[comp][:, 128 * h : 128 * h + 128]
+                shift = (32 * (comp - j)) % 128
+                part = pltpu.roll(part, shift, 1) if shift else part
+                line_ = jnp.where(lax.shift_right_logical(lane, 5) == comp, part, line_)
+            for r in range(ROWS):
+                dsend[r * COLS + c] = line_[r : r + 1, :]
+        me = row * COLS + col
+        for t in range(ROWS - 1, -1, -1):
+            for u in range(COLS - 1, -1, -1):
+                if t or u:
+                    to, at = peer(t), line(u)
+                    remote(dsend.at[to * COLS + at], drecv.at[me], d_send, d_recv, (to, at)).start()
+        drecv[me] = dsend[me]
+
+    def env_total():
+        whole = drecv.at[0 : ROWS * COLS - 1]
+        remote(whole, whole, d_send, d_recv, (row, line(1))).wait_recv()
+        return jnp.sum(drecv[...], axis=0)
 
     def env_middle(buf):
         whole = erecv.at[buf, 0 : ROWS - 1]
@@ -281,23 +322,29 @@
         return (fast_coupling * own_charge) * jnp.concatenate(out, axis=0)
 
     fill_halo(0, spos_ref)
+    wide = jnp.zeros((4, MOL - PIECE), jnp.float32)
+    thin = jnp.zeros((1, PIECE), jnp.float32)
+    for k, ref in enumerate((fpos_ref, fvel_ref)):
+        value = jnp.concatenate([jnp.concatenate([ref[...], thin], axis=0), wide], axis=1)
+        zown[4 * k : 4 * k + 4, :] = pltpu.roll(jnp.concatenate([value, value], axis=0), col * PIECE, 1)[0:4]
     pl.semaphore_wait(barrier, len(partners))
     for t in range(COLS - 1, 0, -1):
-        remote(own_ref, zrecv.at[col], z_send, z_recv, (row, line(t))).start()
+        remote(zown, zrecv.at[col], z_send, z_recv, (row, line(t))).start()
     for d in range(8):
         halo_copy(0, d).start()
-    zrecv[col] = own_ref[...]
+    zrecv[col] = zown[...]
     own_charge = charge_ref[pl.ds(row, 1), :]
-    owner = owner_ref[...]
+    owner = owner_ref[0:1, :]
     corner[0:1, :] = lax.shift_right_logical(owner, 6).astype(jnp.float32)
     corner[1:2, :] = (owner & 63).astype(jnp.float32)
     index = lax.broadcasted_iota(jnp.int32, (ROWS, MOL), 0) * MOL + lax.broadcasted_iota(jnp.int32, (ROWS, MOL), 1)
-    hit = jnp.broadcast_to(excl_ref[0:1, :], (ROWS, MOL)) == index
+    banned = excl_ref[:, pl.ds(pl.multiple_of(row * MOL, MOL), MOL)]
+    hit = jnp.broadcast_to(banned[0:1, :], (ROWS, MOL)) == index
     for e in range(1, 4):
-        hit = hit | (jnp.broadcast_to(excl_ref[e : e + 1, :], (ROWS, MOL)) == index)
+        hit = hit | (jnp.broadcast_to(banned[e : e + 1, :], (ROWS, MOL)) == index)
     barred[...] = jnp.where(hit, charge_ref[...], 0.0)
     fill_table(spos_ref)
-    slow_columns(spos_ref, 0, CELLS)
+    slow_start(spos_ref)
 
     whole = zrecv.at[0 : COLS - 1]
     remote(whole, whole, z_send, z_recv, (row, line(1))).wait_recv()
@@ -309,83 +356,93 @@
     gather_start(0, pos)
     for d in range(8):
         halo_copy(0, d).wait_recv()
-    slow_pairs(0, 0, 12)
+    slow_pairs(0, 0, 18)
     arrivals(0, 1, ROWS)
-    env_start(0)
+    env_rows(0)
     fast_rows(0, 0, ROWS, False)
     force = fast_end(pos)
-    slow_pairs(0, 12, 18)
+    slow_pairs(0, 18, 26)
     env_middle(0)
-    slow_pairs(0, 18, 30)
+    slow_pairs(0, 26, 32)
+    slow_end()
+    for comp in range(3):
+        v = svel_ref[comp] + half_outer * ((slow_coupling * scharge_ref[...]) * sforce[comp])
+        svel_out[comp] = v
+        spos_out[comp] = spos_ref[comp] + outer_dt * v
+    fill_halo(1, spos_out)
+    for d in range(8):
+        halo_copy(1, d).start()
     vel = vel + half_outer * env_end(0)
     for g in range(1, INNER + 1):
         vel = vel + (0.5 * inner_dt) * force
         pos = pos + inner_dt * vel
         gather_start(g, pos)
         if g == 1:
-            slow_pairs(0, 30, 32)
-            slow_sums(0, CELLS)
-            for comp in range(3):
-                v = svel_ref[comp] + half_outer * ((slow_coupling * scharge_ref[...]) * sforce[comp])
-                svel_out[comp] = v
-                spos_out[comp] = spos_ref[comp] + outer_dt * v
-            fill_halo(1, spos_out)
-            for d in range(8):
-                halo_copy(1, d).start()
+            fill_table(spos_out)
+            slow_start(spos_out)
         elif g == 2:
-            slow_columns(spos_out, 0, CELLS)
-            fill_table(spos_out)
-        elif g == 3:
             for d in range(8):
                 halo_copy(1, d).wait_recv()
-            slow_pairs(1, 0, 8)
+            slow_pairs(1, 0, 10)
+        elif g == 3:
+            slow_pairs(1, 10, 20)
         else:
-            slow_pairs(1, 8, 16)
+            slow_pairs(1, 20, 28)
+        fast_rows(g, 0, 1, False)
         if g < INNER:
-            fast_rows(g, 0, 1, False)
             fast_rows(g, 1, ROWS, True)
             force = fast_end(pos)
             vel = vel + (0.5 * inner_dt) * force
         else:
-            fast_rows(g, 0, 1, False)
             fast_rows(g, 1, 12, True)
             arrivals(g, 12, ROWS)
-            env_start(1)
+            env_direct()
             fast_rows(g, 12, ROWS, False)
             force = fast_end(pos)
             vel = vel + (0.5 * inner_dt) * force
-    slow_pairs(1, 16, 26)
-    env_middle(1)
-    slow_pairs(1, 26, 32)
-    slow_sums(0, CELLS)
+    slow_pairs(1, 28, 32)
+    slow_end()
     for comp in range(3):
         svel_out[comp] = svel_out[comp] + half_outer * ((slow_coupling * scharge_ref[...]) * sforce[comp])
-    vel = vel + half_outer * env_end(1)
     back = lax.rem(MOL - col * PIECE, MOL)
-    for value, out in ((pos, fpos_out), (vel, fvel_out)):
-        out[...] = pltpu.roll(jnp.concatenate([value, value], axis=0), back, 1)[0:3, 0:PIECE]
+
+    def own_lanes(value):
+        return pltpu.roll(jnp.concatenate([value, value], axis=0), back, 1)
+
+    fpos_out[...] = own_lanes(pos)[0:3, 0:PIECE]
+    vel = own_lanes(vel)
+    scale = (half_outer * slow_coupling) * own_lanes(jnp.broadcast_to(own_charge, (4, MOL)))[0:1, 0:PIECE]
+    total = env_total()
+    for comp in range(3):
+        part = pltpu.roll(jnp.broadcast_to(total, (8, 128)), 128 - 32 * comp, 1) if comp else total
+        fvel_out[comp : comp + 1, :] = vel[comp : comp + 1, 0:PIECE] + scale * part[0:1, 0:PIECE]
 
     whole = zrecv.at[0 : COLS - 1]
     remote(whole, whole, z_send, z_recv, (row, line(1))).wait_send()
     for buf in range(2):
         for d in range(8):
             halo_copy(buf, d).wait_send()
-        whole = erecv.at[buf, 0 : ROWS - 1]
-        remote(whole, whole, e_send.at[buf], e_recv.at[buf], (row, line(1))).wait_send()
-        whole = zrecv2.at[buf, 0 : COLS - 1]
-        remote(whole, whole, y_send.at[buf], y_recv.at[buf], (row, line(1))).wait_send()
+    for ref, count, send, recv in (
+        (erecv.at[0], ROWS, e_send.at[0], e_recv.at[0]),
+        (zrecv2.at[0], COLS, y_send.at[0], y_recv.at[0]),
+        (drecv, ROWS * COLS, d_send, d_recv),
+    ):
+        whole = ref.at[0 : count - 1]
+        remote(whole, whole, send, recv, (row, line(1))).wait_send()
     for g in range(INNER + 1):
         whole = gath.at[g, 0 : ROWS - 1]
         remote(whole, whole, g_send.at[g], g_recv.at[g, 0], (row, line(1))).wait_send()
 
 
+def finish(*refs):
+    for a, b in zip(refs[:4], refs[4:]):
+        b[...] = a[...]
+
+
 def per_device(fast_pos, fast_vel, fast_charge, fast_owner, exclusions, slow_pos, slow_vel, slow_charge, neighbours):
-    row, col = lax.axis_index("row"), lax.axis_index("col")
-    own = jnp.concatenate([jnp.pad(fast_pos, ((0, 1), (0, 0))), jnp.pad(fast_vel, ((0, 1), (0, 0)))], axis=0)
-    own = lax.dynamic_update_slice(jnp.zeros((8, MOL), jnp.float32), own, (0, col * PIECE))
     charge = fast_charge.reshape(ROWS, MOL)
-    owner = fast_owner[:MOL].reshape(1, MOL)
-    excl = lax.dynamic_slice(exclusions, (row * MOL, 0), (MOL, 4)).T
+    owner = fast_owner.reshape(ROWS, MOL)
+    excl = exclusions.T
     f32 = jnp.float32
     vmem = pl.BlockSpec(memory_space=pltpu.VMEM)
     dma = pltpu.SemaphoreType.DMA
@@ -397,7 +454,7 @@
             jax.ShapeDtypeStruct((3, CELLS, CELL), f32),
             jax.ShapeDtypeStruct((3, CELLS, CELL), f32),
         ),
-        in_specs=[vmem] * 7 + [pl.BlockSpec(memory_space=pltpu.SMEM)],
+        in_specs=[vmem] * 8 + [pl.BlockSpec(memory_space=pltpu.SMEM)],
         out_specs=(vmem,) * 4,
         scratch_shapes=[
             pltpu.VMEM((COLS, 8, MOL), f32),
@@ -411,10 +468,15 @@
             pltpu.VMEM((3, MOL, 128), f32),
             pltpu.VMEM((CR + 4, CC + 4, 4, CELL), f32),
             pltpu.VMEM((CR + 4, CC + 4, 4, CELL), f32),
-            pltpu.VMEM((CELLS, 3, CELL, CELL), f32),
-            pltpu.VMEM((CELLS, 3, CELL, CELL), f32),
+            pltpu.VMEM((3, CELL, CELL), f32),
+            pltpu.VMEM((3, CELL, CELL), f32),
+            pltpu.VMEM((3, CELL, CELL), f32),
+            pltpu.VMEM((3, CELL, CELL), f32),
             pltpu.VMEM((3, CELLS, CELL), f32),
             pltpu.VMEM((4 * CELL, MOL), f32),
+            pltpu.VMEM((8, MOL), f32),
+            pltpu.VMEM((ROWS * COLS, 1, 128), f32),
+            pltpu.VMEM((ROWS * COLS, 1, 128), f32),
             pltpu.VMEM((2, MOL), f32),
             pltpu.VMEM((ROWS, MOL), f32),
             dma,
@@ -427,20 +489,26 @@
             dma((2,)),
             dma((2, 8)),
             dma((2, 8)),
+            dma,
+            dma,
         ],
         compiler_params=pltpu.CompilerParams(
-            collective_id=0, has_side_effects=True, vmem_limit_bytes=40 * 1024 * 1024
+            collective_id=0, has_side_effects=True, vmem_limit_bytes=24 * 1024 * 1024
         ),
     )(
-        own,
+        fast_pos,
+        fast_vel,
         charge,
         owner,
         excl,
         slow_pos.reshape(3, CELLS, CELL),
         slow_vel.reshape(3, CELLS, CELL),
         slow_charge.reshape(CELLS, CELL),
-        neighbours.reshape(CELLS, NBR),
+        neighbours.transpose(2, 0, 1),
     )
+    outs = pl.pallas_call(
+        finish, out_shape=[jax.ShapeDtypeStruct(o.shape, f32) for o in outs], in_specs=[vmem] * 4, out_specs=[vmem] * 4
+    )(*outs)
     fpos, fvel, spos, svel = outs
     return fpos, fvel, spos.reshape(3, CR, CC, CELL), svel.reshape(3, CR, CC, CELL)
 

time: 76.6 us -> 73.4 us (0.958); the launches traced: 76.4 us -> 72.3 us
  Pallas kernels: 70.7 us -> 65.2 us
  local copies, waits for them, and re-layouts: 4.27 us -> 6.34 us
    pallas_call x1, Pallas kernels: 70.7 us -> 63.8 us  [per_device(): pl.pallas_call(kernel, out_shape=(jax.ShapeDtypeStruct((3, PIECE), f32),...]
    unnamed x17 -> x22, local copies, waits for them, and re-layouts: 3.27 us -> 4.83 us
    pallas_call x0 -> x1, Pallas kernels: none -> 1.48 us  [per_device(): pl.pallas_call(finish, out_shape=[jax.ShapeDtypeStruct(o.shape, f32) for...]
where the time goes in v1:
time: 73.4 us; the launch traced here: 72.3 us
  Pallas kernels  65.2 us (89%)
  local copies, waits for them, and re-layouts  6.34 us (9%)
    pallas_call x1, Pallas kernels, per_device(): pl.pallas_call(kernel, out_shape=(jax.ShapeDtypeStruct((3, PIECE), f32),...  63.8 us
    unnamed x22, local copies, waits for them, and re-layouts  4.83 us
    pallas_call x1, Pallas kernels, per_device(): pl.pallas_call(finish, out_shape=[jax.ShapeDtypeStruct(o.shape, f32) for...  1.48 us

profile of v1, /device:TPU:0, one launch (start us, length us, event | category | flops | bytes accessed | tf_op | source)
XLA Modules:
  0.0 72.3 jit_solution(7263978772559066124)
XLA Ops:
  0.6 0.0 copy-start
  0.6 0.8 %reshape.29.charge_ref = f32[16,256]{1,0:T(8,128)S(1)} reshape(f32[4096]{0:T(1024)} %param.11) | data formatting | bytes 32768 | tf_op jit(solution)/shard_map/reshape | solution.py:443
  1.4 0.0 copy-start.7
  1.4 0.0 copy-start.8
  1.4 0.7 %reshape.30.owner_ref = s32[16,256]{1,0:T(8,128)S(1)} reshape(s32[4096]{0:T(1024)} %param.12) | data formatting | bytes 32768 | tf_op jit(solution)/shard_map/reshape | solution.py:444
  2.1 0.0 copy-done
  2.2 0.0 copy-done.7
  2.2 0.0 copy-done.8
  2.2 0.0 copy-start.1
  2.2 0.8 %copy-done.1 = f32[3,4,8,128]{3,2,1,0:T(8,128)S(1)} copy-done((f32[3,4,8,128]{3,2,1,0:T(8,128)S(1)}, f32[3,4,8,128]{3,2,1,0:T(8,128)}, u32[]{:S(2)}) %copy-start.1) | copy-done | bytes 49176
  3.0 0.0 copy-start.2
  3.0 0.8 %copy-done.2 = f32[3,4,8,128]{3,2,1,0:T(8,128)S(1)} copy-done((f32[3,4,8,128]{3,2,1,0:T(8,128)S(1)}, f32[3,4,8,128]{3,2,1,0:T(8,128)}, u32[]{:S(2)}) %copy-start.2) | copy-done | bytes 49176
  3.8 0.0 copy-start.5
  3.8 0.7 copy-done.5
  4.5 0.0 copy-start.6
  4.5 0.7 copy-done.6
  5.2 63.8 %shard_map.120 = (f32[3,32]{1,0:T(4,128)S(1)}, f32[3,32]{1,0:T(4,128)S(1)}, f32[3,32,128]{2,1,0:T(8,128)S(1)}, f32[3,32,128]{2,1,0:T(8,128)S(1)}) custom-call(f32[3,32]{1,0:T(4,128)S(1)} %copy-done.7, f32[3,32]{1,0:T(4,128)S(1)} %copy-done.8, f32[16,256]{1,0:T(8,128)S(1)} %reshape.29.charge_ref, s32[16,256]{1,0:T(8,128)S(1)} %reshape.30.owner_ref, ...), custom_call_target="tpu_custom_call" | custom-call | tf_op jit(solution)/shard_map/pallas_call | solution.py:449
  69.0 0.0 copy-start.3
  69.0 0.6 copy-done.3
  69.6 0.0 copy-start.4
  69.6 0.6 copy-done.4
  70.2 0.6 copy-done.9
  70.8 0.0 copy-done.10
  70.8 1.5 %shard_map.121 = (f32[3,32]{1,0:T(4,128)}, f32[3,32]{1,0:T(4,128)}, f32[3,32,128]{2,1,0:T(8,128)}, f32[3,32,128]{2,1,0:T(8,128)}) custom-call(f32[3,32]{1,0:T(4,128)} %copy-done.9, f32[3,32]{1,0:T(4,128)} %copy-done.10, f32[3,32,128]{2,1,0:T(8,128)} %copy-done.3, f32[3,32,128]{2,1,0:T(8,128)} %copy-done.4), custom_call_target="tpu_custom_call" | custom-call | tf_op jit(solution)/shard_map/pallas_call | solution.py:509
  (2 shorter events, 0.0 us)
Async XLA Ops:
  0.6 1.5 %copy-start = (s32[4096,4]{0,1:T(4,128)S(1)}, s32[4096,4]{0,1:T(4,128)}, u32[]{:S(2)}) copy-start(s32[4096,4]{0,1:T(4,128)} %param.13) | copy-start | bytes 196612
  1.4 0.8 %copy-start.7 = (f32[3,32]{1,0:T(4,128)S(1)}, f32[3,32]{1,0:T(4,128)}, u32[]{:S(2)}) copy-start(f32[3,32]{1,0:T(4,128)} %fpos_ref.1) | copy-start | bytes 1156
  1.4 0.8 %copy-start.8 = (f32[3,32]{1,0:T(4,128)S(1)}, f32[3,32]{1,0:T(4,128)}, u32[]{:S(2)}) copy-start(f32[3,32]{1,0:T(4,128)} %fvel_ref.1) | copy-start | bytes 1156
  2.2 0.8 %copy-start.1 = (f32[3,4,8,128]{3,2,1,0:T(8,128)S(1)}, f32[3,4,8,128]{3,2,1,0:T(8,128)}, u32[]{:S(2)}) copy-start(f32[3,4,8,128]{3,2,1,0:T(8,128)} %param.14) | copy-start | bytes 147460
  3.0 0.8 %copy-start.2 = (f32[3,4,8,128]{3,2,1,0:T(8,128)S(1)}, f32[3,4,8,128]{3,2,1,0:T(8,128)}, u32[]{:S(2)}) copy-start(f32[3,4,8,128]{3,2,1,0:T(8,128)} %param.15) | copy-start | bytes 147460
  3.8 0.7 copy-start.5
  4.5 0.7 copy-start.6
  69.0 0.6 copy-start.3
  69.6 0.6 copy-start.4
  70.2 0.6 copy-start.9
  70.2 0.6 copy-start.10

commit v2 on v1

--- a/solution.py
+++ b/solution.py
@@ -15,7 +15,9 @@
 PIECE = MOL // COLS
 CR, CC = 4, 8
 CELLS = CR * CC
-TOTAL_COLS = 64
+VMEM = 67043328
+
+ORDER = (0, 1, 3, 4, 12, 2, 8, 5, 7, 13, 15, 6, 14, 9, 11, 10)
 
 fast_coupling = 1.0
 slow_coupling = 0.1
@@ -31,8 +33,9 @@
 
 
 def kernel(
-    fpos_ref, fvel_ref, charge_ref, owner_ref, excl_ref, spos_ref, svel_ref, scharge_ref, nbr_ref,
+    fpos_in, fvel_in, charge_in, owner_in, excl_in, spos_in, svel_in, scharge_in, nbr_in,
     fpos_out, fvel_out, spos_out, svel_out,
+    fpos_ref, fvel_ref, charge_raw, owner_ref, excl_ref, spos_ref, svel_ref, scharge_ref, nbr_ref, charge_ref, in_sem,
     zrecv, gath, mat, esend, erecv, zsend2, zrecv2, acol, facc, halo_0, halo_1, scol_0, scol_1, sacc_0, sacc_1, sforce, table, zown, dsend, drecv, corner, barred,
     z_send, z_recv, g_send, g_recv, e_send, e_recv, y_send, y_recv, h_send, h_recv, d_send, d_recv,
 ):
@@ -41,14 +44,15 @@
     halos = (halo_0, halo_1)
     px, py = lax.div(row, 4), lax.rem(row, 4)
 
-    def turn(u):
-        return u + lax.div(u, 2) * (5 - 2 * u)
-
     def peer(t):
         if isinstance(t, int):
-            dx, dy = (0, 1, 3, 2)[t // 4], (0, 1, 3, 2)[t % 4]
+            code = ORDER[t]
+            dx, dy = code // 4, code % 4
         else:
-            dx, dy = turn(lax.div(t, 4)), turn(lax.rem(t, 4))
+            code = jnp.int32(0)
+            for k in range(1, ROWS):
+                code = jnp.where(t == k, ORDER[k], code)
+            dx, dy = lax.div(code, 4), lax.rem(code, 4)
         return lax.rem(px + dx, 4) * 4 + lax.rem(py + dy, 4)
 
     def line(t):
@@ -61,6 +65,25 @@
         return pltpu.make_async_remote_copy(
             src_ref=src, dst_ref=dst, send_sem=send, recv_sem=recv, device_id=to, device_id_type=MESH
         )
+
+    loads = [
+        pltpu.make_async_copy(src, dst, in_sem.at[k])
+        for k, (src, dst) in enumerate(
+            (
+                (spos_in, spos_ref),
+                (scharge_in, scharge_ref),
+                (fpos_in, fpos_ref),
+                (fvel_in, fvel_ref),
+                (charge_in, charge_raw),
+                (owner_in.at[0:8], owner_ref),
+                (excl_in.at[:, pl.ds(pl.multiple_of(row * MOL, MOL), MOL)], excl_ref),
+                (nbr_in, nbr_ref),
+                (svel_in, svel_ref),
+            )
+        )
+    ]
+    for load in loads:
+        load.start()
 
     barrier = pltpu.get_barrier_semaphore()
     partners = [(peer(t), col) for t in range(1, ROWS)] + [(row, line(t)) for t in range(1, COLS)]
@@ -153,8 +176,11 @@
     def slow_end():
         slow_sums(CELLS - 1, sacc_1)
 
+    def owner_line():
+        return jnp.concatenate([owner_ref[0:1, :], owner_ref[1:2, :]], axis=1)
+
     def fill_table(pos):
-        owner = owner_ref[0:1, :]
+        owner = owner_line()
         gr = lax.shift_right_logical(owner, 6) - row * CR
         gc = (owner & 63) - col * CC
         inside = (gr >= 0) & (gr < CR) & (gc >= 0) & (gc < CC)
@@ -321,7 +347,11 @@
         out.append(jnp.zeros((1, MOL), jnp.float32))
         return (fast_coupling * own_charge) * jnp.concatenate(out, axis=0)
 
+    loads[0].wait()
+    loads[1].wait()
     fill_halo(0, spos_ref)
+    loads[2].wait()
+    loads[3].wait()
     wide = jnp.zeros((4, MOL - PIECE), jnp.float32)
     thin = jnp.zeros((1, PIECE), jnp.float32)
     for k, ref in enumerate((fpos_ref, fvel_ref)):
@@ -333,12 +363,16 @@
     for d in range(8):
         halo_copy(0, d).start()
     zrecv[col] = zown[...]
+    for load in loads[4:]:
+        load.wait()
+    for h in range(2):
+        charge_ref[:, 128 * h : 128 * h + 128] = charge_raw[pl.ds(h, ROWS, stride=2), :]
     own_charge = charge_ref[pl.ds(row, 1), :]
-    owner = owner_ref[0:1, :]
+    owner = owner_line()
     corner[0:1, :] = lax.shift_right_logical(owner, 6).astype(jnp.float32)
     corner[1:2, :] = (owner & 63).astype(jnp.float32)
     index = lax.broadcasted_iota(jnp.int32, (ROWS, MOL), 0) * MOL + lax.broadcasted_iota(jnp.int32, (ROWS, MOL), 1)
-    banned = excl_ref[:, pl.ds(pl.multiple_of(row * MOL, MOL), MOL)]
+    banned = excl_ref[...]
     hit = jnp.broadcast_to(banned[0:1, :], (ROWS, MOL)) == index
     for e in range(1, 4):
         hit = hit | (jnp.broadcast_to(banned[e : e + 1, :], (ROWS, MOL)) == index)
@@ -361,9 +395,9 @@
     env_rows(0)
     fast_rows(0, 0, ROWS, False)
     force = fast_end(pos)
-    slow_pairs(0, 18, 26)
+    slow_pairs(0, 18, 22)
     env_middle(0)
-    slow_pairs(0, 26, 32)
+    slow_pairs(0, 22, 32)
     slow_end()
     for comp in range(3):
         v = svel_ref[comp] + half_outer * ((slow_coupling * scharge_ref[...]) * sforce[comp])
@@ -383,11 +417,11 @@
         elif g == 2:
             for d in range(8):
                 halo_copy(1, d).wait_recv()
-            slow_pairs(1, 0, 10)
+            slow_pairs(1, 0, 6)
         elif g == 3:
-            slow_pairs(1, 10, 20)
+            slow_pairs(1, 6, 12)
         else:
-            slow_pairs(1, 20, 28)
+            slow_pairs(1, 12, 18)
         fast_rows(g, 0, 1, False)
         if g < INNER:
             fast_rows(g, 1, ROWS, True)
@@ -400,7 +434,7 @@
             fast_rows(g, 12, ROWS, False)
             force = fast_end(pos)
             vel = vel + (0.5 * inner_dt) * force
-    slow_pairs(1, 28, 32)
+    slow_pairs(1, 18, 32)
     slow_end()
     for comp in range(3):
         svel_out[comp] = svel_out[comp] + half_outer * ((slow_coupling * scharge_ref[...]) * sforce[comp])
@@ -440,11 +474,12 @@
 
 
 def per_device(fast_pos, fast_vel, fast_charge, fast_owner, exclusions, slow_pos, slow_vel, slow_charge, neighbours):
-    charge = fast_charge.reshape(ROWS, MOL)
-    owner = fast_owner.reshape(ROWS, MOL)
+    charge = fast_charge.reshape(FAST // 128, 128)
+    owner = fast_owner.reshape(FAST // 128, 128)
     excl = exclusions.T
     f32 = jnp.float32
     vmem = pl.BlockSpec(memory_space=pltpu.VMEM)
+    hbm = pl.BlockSpec(memory_space=pltpu.HBM)
     dma = pltpu.SemaphoreType.DMA
     outs = pl.pallas_call(
         kernel,
@@ -454,9 +489,20 @@
             jax.ShapeDtypeStruct((3, CELLS, CELL), f32),
             jax.ShapeDtypeStruct((3, CELLS, CELL), f32),
         ),
-        in_specs=[vmem] * 8 + [pl.BlockSpec(memory_space=pltpu.SMEM)],
+        in_specs=[hbm] * 9,
         out_specs=(vmem,) * 4,
         scratch_shapes=[
+            pltpu.VMEM((3, PIECE), f32),
+            pltpu.VMEM((3, PIECE), f32),
+            pltpu.VMEM((FAST // 128, 128), f32),
+            pltpu.VMEM((8, 128), jnp.int32),
+            pltpu.VMEM((4, MOL), jnp.int32),
+            pltpu.VMEM((3, CELLS, CELL), f32),
+            pltpu.VMEM((3, CELLS, CELL), f32),
+            pltpu.VMEM((CELLS, CELL), f32),
+            pltpu.SMEM((NBR, CR, CC), jnp.int32),
+            pltpu.VMEM((ROWS, MOL), f32),
+            dma((9,)),
             pltpu.VMEM((COLS, 8, MOL), f32),
             pltpu.VMEM((INNER + 1, ROWS, 4, MOL), f32),
             pltpu.VMEM((3, ROWS, MOL), f32),
@@ -493,7 +539,7 @@
             dma,
         ],
         compiler_params=pltpu.CompilerParams(
-            collective_id=0, has_side_effects=True, vmem_limit_bytes=24 * 1024 * 1024
+            collective_id=0, has_side_effects=True, vmem_limit_bytes=VMEM
         ),
     )(
         fast_pos,
@@ -507,7 +553,8 @@
         neighbours.transpose(2, 0, 1),
     )
     outs = pl.pallas_call(
-        finish, out_shape=[jax.ShapeDtypeStruct(o.shape, f32) for o in outs], in_specs=[vmem] * 4, out_specs=[vmem] * 4
+        finish, out_shape=[jax.ShapeDtypeStruct(o.shape, f32) for o in outs], in_specs=[vmem] * 4, out_specs=[vmem] * 4,
+        compiler_params=pltpu.CompilerParams(vmem_limit_bytes=VMEM),
     )(*outs)
     fpos, fvel, spos, svel = outs
     return fpos, fvel, spos.reshape(3, CR, CC, CELL), svel.reshape(3, CR, CC, CELL)

time: 73.4 us -> 65.7 us (0.90)
  local copies, waits for them, and re-layouts: 6.34 us -> 0 us
  Pallas kernels: 65.2 us -> 64.3 us
    unnamed x22 -> x0, local copies, waits for them, and re-layouts: 4.83 us -> none
    reshape x2 -> x0, local copies, waits for them, and re-layouts: 1.5 us -> none  [the longest x1 0.75 us: per_device(): charge = fast_charge.reshape(ROWS, MOL)]
    pallas_call x1, Pallas kernels: 63.8 us -> 62.9 us  [per_device(): pl.pallas_call(kernel, out_shape=(jax.ShapeDtypeStruct((3, PIECE), f32),...]
where the time goes in v2:
time: 65.7 us; the launch traced here: 65 us
  Pallas kernels  64.3 us (98%)
    pallas_call x1, Pallas kernels, per_device(): pl.pallas_call(kernel, out_shape=(jax.ShapeDtypeStruct((3, PIECE), f32),...  62.9 us
    pallas_call x1, Pallas kernels, per_device(): pl.pallas_call(finish, out_shape=[jax.ShapeDtypeStruct(o.shape, f32) for...  1.48 us

profile of v2, /device:TPU:0, one launch (start us, length us, event | category | flops | bytes accessed | tf_op | source)
XLA Modules:
  0.0 65.0 jit_solution(4292587144471550286)
XLA Ops:
  0.6 62.9 %shard_map.120 = (f32[3,32]{1,0:T(4,128)}, f32[3,32]{1,0:T(4,128)}, f32[3,32,128]{2,1,0:T(8,128)}, f32[3,32,128]{2,1,0:T(8,128)}) custom-call(f32[3,32]{1,0:T(4,128)} %fpos_in.1, f32[3,32]{1,0:T(4,128)} %fvel_in.1, f32[32,128]{1,0:T(8,128)} %bitcast.12, s32[32,128]{1,0:T(8,128)} %bitcast.13, s32[4,4096]{1,0:T(4,128)} %bitcast.9, f32[3,32,128]{2,1,0:T(8,128)} %bitcast.10, ...), custom_call_target="tpu_custom_call" | custom-call | tf_op jit(solution)/shard_map/pallas_call | solution.py:484
  63.5 1.5 %shard_map.121 = (f32[3,32]{1,0:T(4,128)}, f32[3,32]{1,0:T(4,128)}, f32[3,32,128]{2,1,0:T(8,128)}, f32[3,32,128]{2,1,0:T(8,128)}) custom-call(f32[3,32]{1,0:T(4,128)} %get-tuple-element.12.refs_0_, f32[3,32]{1,0:T(4,128)} %get-tuple-element.13.refs_1_, f32[3,32,128]{2,1,0:T(8,128)} %get-tuple-element.14.refs_2_, f32[3,32,128]{2,1,0:T(8,128)} %get-tuple-element.15.refs_3_), custom_call_target="tpu_custom_call" | custom-call | tf_op jit(solution)/shard_map/pallas_call | solution.py:555

commit v3 on v2

--- a/solution.py
+++ b/solution.py
@@ -18,6 +18,8 @@
 VMEM = 67043328
 
 ORDER = (0, 1, 3, 4, 12, 2, 8, 5, 7, 13, 15, 6, 14, 9, 11, 10)
+LINE = 4
+HOPS = (2, 1, 3, 0)
 
 fast_coupling = 1.0
 slow_coupling = 0.1
@@ -36,13 +38,13 @@
     fpos_in, fvel_in, charge_in, owner_in, excl_in, spos_in, svel_in, scharge_in, nbr_in,
     fpos_out, fvel_out, spos_out, svel_out,
     fpos_ref, fvel_ref, charge_raw, owner_ref, excl_ref, spos_ref, svel_ref, scharge_ref, nbr_ref, charge_ref, in_sem,
-    zrecv, gath, mat, esend, erecv, zsend2, zrecv2, acol, facc, halo_0, halo_1, scol_0, scol_1, sacc_0, sacc_1, sforce, table, zown, dsend, drecv, corner, barred,
-    z_send, z_recv, g_send, g_recv, e_send, e_recv, y_send, y_recv, h_send, h_recv, d_send, d_recv,
+    psend, precv, vsend, vrecv, gath, mat, esend, erecv, zsend2, zrecv2, acol, facc, halo_0, halo_1, scol_0, scol_1, sacc_0, sacc_1, sforce, table, dsend, drecv, corner, barred,
+    p_send, p_recv, v_send, v_recv, g_send, g_recv, e_send, e_recv, y_send, y_recv, h_send, h_recv, d_send, d_recv,
 ):
     row = lax.axis_index("row")
     col = lax.axis_index("col")
     halos = (halo_0, halo_1)
-    px, py = lax.div(row, 4), lax.rem(row, 4)
+    px, py, pz, pk = lax.div(row, 4), lax.rem(row, 4), lax.div(col, 2), lax.rem(col, 2)
 
     def peer(t):
         if isinstance(t, int):
@@ -50,13 +52,31 @@
             dx, dy = code // 4, code % 4
         else:
             code = jnp.int32(0)
-            for k in range(1, ROWS):
-                code = jnp.where(t == k, ORDER[k], code)
+            for n in range(1, ROWS):
+                code = jnp.where(t == n, ORDER[n], code)
             dx, dy = lax.div(code, 4), lax.rem(code, 4)
         return lax.rem(px + dx, 4) * 4 + lax.rem(py + dy, 4)
 
+    def plane():
+        for t in range(ROWS - 1, -1, -1):
+            for k in (1 - pk, pk) if t else (1 - pk,):
+                r = peer(t)
+                yield (r, pz * 2 + k), r, k
+
     def line(t):
-        return lax.rem(col + t, COLS)
+        return row, lax.rem(pz + t, LINE) * 2 + pk
+
+    def everyone():
+        for dx in HOPS:
+            for dy in HOPS:
+                for dz in HOPS:
+                    for dk in (1, 0):
+                        if dx or dy or dz or dk:
+                            r = lax.rem(px + dx, 4) * 4 + lax.rem(py + dy, 4)
+                            z, k = lax.rem(pz + dz, 4), lax.rem(pk + dk, 2)
+                            yield (r, z * 2 + k), (k * 4 + z) * ROWS + r
+
+    mine = (pk * 4 + pz) * ROWS + row
 
     def side(a, b):
         return lax.rem(row + (a + ROWS), ROWS), lax.rem(col + (b + COLS), COLS)
@@ -86,10 +106,22 @@
         load.start()
 
     barrier = pltpu.get_barrier_semaphore()
-    partners = [(peer(t), col) for t in range(1, ROWS)] + [(row, line(t)) for t in range(1, COLS)]
-    partners += [side(a, b) for a, b in SIDES if a and b]
-    for to in partners:
+    for to, _ in everyone():
         pl.semaphore_signal(barrier, inc=1, device_id=to, device_id_type=MESH)
+
+    def ordered(value):
+        lane = lax.shift_right_logical(lax.broadcasted_iota(jnp.int32, (value.shape[0], 128), 1), 5)
+        halves = []
+        for k in range(2):
+            out = None
+            for z in range(4):
+                c = 2 * z + k
+                part = value[:, 128 * (c // 4) : 128 * (c // 4) + 128]
+                shift = 32 * ((z - c) % 4)
+                part = pltpu.roll(part, shift, 1) if shift else part
+                out = part if out is None else jnp.where(lane == z, part, out)
+            halves.append(out)
+        return jnp.concatenate(halves, axis=1)
 
     def fill_halo(buf, pos):
         for r in range(CR):
@@ -177,7 +209,8 @@
         slow_sums(CELLS - 1, sacc_1)
 
     def owner_line():
-        return jnp.concatenate([owner_ref[0:1, :], owner_ref[1:2, :]], axis=1)
+        line_ = jnp.concatenate([owner_ref[0:1, :], owner_ref[1:2, :]], axis=1)
+        return ordered(jnp.broadcast_to(line_, (8, MOL)))[0:1]
 
     def fill_table(pos):
         owner = owner_line()
@@ -194,7 +227,7 @@
             )
 
     def env_partial():
-        mx, my, mz = mat[0], mat[1], mat[2]
+        mx, my, mz = (jnp.concatenate([mat[comp, 0], mat[comp, 1]], axis=1) for comp in range(3))
 
         def body(jb, carry):
             fx, fy, fz = carry
@@ -213,16 +246,16 @@
         zero = jnp.zeros((ROWS, MOL), jnp.float32)
         return lax.fori_loop(0, CELL // 4, body, (zero, zero, zero))
 
-    def env_rows(buf):
+    def env_rows():
         force = env_partial()
         for r in range(ROWS):
-            for comp in range(3):
-                esend[buf, r, comp : comp + 1, :] = force[comp][r : r + 1, :]
-            esend[buf, r, 3:4, :] = jnp.zeros((1, MOL), jnp.float32)
-        for t in range(ROWS - 1, 0, -1):
-            to = peer(t)
-            remote(esend.at[buf, to], erecv.at[buf, row], e_send.at[buf], e_recv.at[buf], (to, col)).start()
-        erecv[buf, row] = esend[buf, row]
+            for k in range(2):
+                for comp in range(3):
+                    esend[r, k, comp : comp + 1, :] = force[comp][r : r + 1, 128 * k : 128 * k + 128]
+                esend[r, k, 3:4, :] = jnp.zeros((1, 128), jnp.float32)
+        for to, r, k in plane():
+            remote(esend.at[r, k], erecv.at[row * 2 + pk], e_send, e_recv, to).start()
+        erecv[row * 2 + pk] = esend[row, pk]
 
     def env_direct():
         force = env_partial()
@@ -236,70 +269,73 @@
                 part = pltpu.roll(part, shift, 1) if shift else part
                 line_ = jnp.where(lax.shift_right_logical(lane, 5) == comp, part, line_)
             for r in range(ROWS):
-                dsend[r * COLS + c] = line_[r : r + 1, :]
-        me = row * COLS + col
-        for t in range(ROWS - 1, -1, -1):
-            for u in range(COLS - 1, -1, -1):
-                if t or u:
-                    to, at = peer(t), line(u)
-                    remote(dsend.at[to * COLS + at], drecv.at[me], d_send, d_recv, (to, at)).start()
-        drecv[me] = dsend[me]
+                dsend[c * ROWS + r] = line_[r : r + 1, :]
+        for to, slot in everyone():
+            remote(dsend.at[slot], drecv.at[mine], d_send, d_recv, to).start()
+        drecv[mine] = dsend[mine]
 
     def env_total():
         whole = drecv.at[0 : ROWS * COLS - 1]
-        remote(whole, whole, d_send, d_recv, (row, line(1))).wait_recv()
+        remote(whole, whole, d_send, d_recv, line(1)).wait_recv()
         return jnp.sum(drecv[...], axis=0)
 
-    def env_middle(buf):
-        whole = erecv.at[buf, 0 : ROWS - 1]
-        remote(whole, whole, e_send.at[buf], e_recv.at[buf], (row, line(1))).wait_recv()
-        total = erecv[buf, 0]
-        for r in range(1, ROWS):
-            total = total + erecv[buf, r]
-        zsend2[buf] = total
-        for t in range(COLS - 1, 0, -1):
-            remote(zsend2.at[buf], zrecv2.at[buf, col], y_send.at[buf], y_recv.at[buf], (row, line(t))).start()
-        zrecv2[buf, col] = total
-
-    def env_end(buf):
-        whole = zrecv2.at[buf, 0 : COLS - 1]
-        remote(whole, whole, y_send.at[buf], y_recv.at[buf], (row, line(1))).wait_recv()
-        total = zrecv2[buf, 0]
-        for c in range(1, COLS):
-            total = total + zrecv2[buf, c]
-        return (slow_coupling * own_charge) * total
+    def env_middle():
+        whole = erecv.at[0 : 2 * ROWS - 1]
+        remote(whole, whole, e_send, e_recv, line(1)).wait_recv()
+        zsend2[...] = jnp.sum(erecv[...], axis=0)
+        for t in (2, 1, 3):
+            remote(zsend2, zrecv2.at[pz], y_send, y_recv, line(t)).start()
+        zrecv2[pz] = zsend2[...]
+
+    def env_end():
+        whole = zrecv2.at[0 : LINE - 1]
+        remote(whole, whole, y_send, y_recv, line(1)).wait_recv()
+        return (slow_coupling * own_charge) * jnp.sum(zrecv2[...], axis=0)
 
     def gather_start(g, pos):
-        gath[g, row] = pos
-        for t in range(ROWS - 1, 0, -1):
-            remote(gath.at[g, row], gath.at[g, row], g_send.at[g], g_recv.at[g, row], (peer(t), col)).start()
+        gath[g, row, pk] = pos
+        for to, r, k in plane():
+            slot = gath.at[g, row, pk]
+            remote(slot, slot, g_send.at[g], g_recv.at[g, row], to).start()
+        for comp in range(3):
+            mat[comp, pk, pl.ds(row, 1), :] = pos[comp : comp + 1, :]
+        own_columns(pos)
+
+    def own_columns(pos):
         for comp in range(3):
             line_ = pos[comp : comp + 1, :]
-            mat[comp, pl.ds(row, 1), :] = line_
             if comp < 2:
-                line_ = line_ + corner[comp : comp + 1, :]
-            for h in range(2):
-                acol[comp, 128 * h : 128 * h + 128, :] = column(line_[:, 128 * h : 128 * h + 128])
+                line_ = line_ + corner[comp, pk]
+            acol[comp] = column(line_)
         facc[...] = jnp.zeros_like(facc)
 
     def arrive(g, t):
         r = peer(t)
         slot = gath.at[g, r]
-        remote(slot, slot, g_send.at[g], g_recv.at[g, r], (r, col)).wait_recv()
+        remote(slot, slot, g_send.at[g], g_recv.at[g, r], line(1)).wait_recv()
+        for k in range(2):
+            for comp in range(3):
+                mat[comp, k, pl.ds(r, 1), :] = gath[g, r, k, comp : comp + 1, :]
+
+    def arrive_core(g):
+        slot = gath.at[g, row, 1 - pk]
+        remote(slot, slot, g_send.at[g], g_recv.at[g, row], line(1)).wait_recv()
         for comp in range(3):
-            mat[comp, pl.ds(r, 1), :] = gath[g, r, comp : comp + 1, :]
+            mat[comp, 1 - pk, pl.ds(row, 1), :] = gath[g, row, 1 - pk, comp : comp + 1, :]
 
     def fast_row(g, t):
         r = peer(t)
-        tile = gath[g, r]
-        lines = (
-            tile[0:1] + corner[0:1, :],
-            tile[1:2] + corner[1:2, :],
-            tile[2:3],
-            charge_ref[pl.ds(r, 1), :],
-        )
-        halves = [[jnp.broadcast_to(v[:, 128 * h : 128 * h + 128], (8, 128)) for v in lines] for h in range(2)]
-        for i in range(MOL // 8):
+        halves = [
+            (
+                mat[0, h, pl.ds(r, 1), :] + corner[0, h],
+                mat[1, h, pl.ds(r, 1), :] + corner[1, h],
+                mat[2, h, pl.ds(r, 1), :],
+                charge_ref[h, pl.ds(r, 1), :],
+            )
+            for h in range(2)
+        ]
+        halves = [[jnp.broadcast_to(v, (8, 128)) for v in lines] for lines in halves]
+        for i in range(16):
             x = acol[0, 8 * i : 8 * i + 8, :]
             y = acol[1, 8 * i : 8 * i + 8, :]
             z = acol[2, 8 * i : 8 * i + 8, :]
@@ -333,95 +369,125 @@
         lax.fori_loop(t0, t1, body, 0)
 
     def fast_end(pos):
-        d = [jnp.broadcast_to(pos[comp : comp + 1, :], (ROWS, MOL)) - mat[comp] for comp in range(3)]
+        d = [jnp.broadcast_to(pos[comp : comp + 1, :], (ROWS, 128)) - mat[comp, pk] for comp in range(3)]
         s = (d[0] * d[0] + d[1] * d[1]) + (d[2] * d[2] + 1.0)
         inv = lax.rsqrt(s)
         w = (inv * inv) * (inv * barred[...])
         out = []
         for comp in range(3):
-            parts = [
-                jnp.sum(jnp.transpose(facc[comp, 128 * h : 128 * h + 128, :]), axis=0, keepdims=True) for h in range(2)
-            ]
-            total = jnp.concatenate(parts, axis=1)
+            total = jnp.sum(jnp.transpose(facc[comp]), axis=0, keepdims=True)
             out.append(total - jnp.sum(w * d[comp], axis=0, keepdims=True))
-        out.append(jnp.zeros((1, MOL), jnp.float32))
+        out.append(jnp.zeros((1, 128), jnp.float32))
         return (fast_coupling * own_charge) * jnp.concatenate(out, axis=0)
 
+    def packed(ref):
+        value = jnp.concatenate([ref[...], jnp.zeros((3, 128 - PIECE), jnp.float32)], axis=1)
+        out = jnp.broadcast_to(value[0:1], (8, 128))
+        for comp in (1, 2):
+            out = out + pltpu.roll(jnp.broadcast_to(value[comp : comp + 1], (8, 128)), PIECE * comp, 1)
+        return out[0:1]
+
+    loads[2].wait()
+    loads[3].wait()
+    psend[...] = packed(fpos_ref)
+    vsend[...] = packed(fvel_ref)
+    precv[mine] = psend[...]
+    vrecv[pz] = vsend[...]
+    pl.semaphore_wait(barrier, ROWS * COLS - 1)
+    for to, _ in everyone():
+        remote(psend, precv.at[mine], p_send, p_recv, to).start()
     loads[0].wait()
     loads[1].wait()
     fill_halo(0, spos_ref)
-    loads[2].wait()
-    loads[3].wait()
-    wide = jnp.zeros((4, MOL - PIECE), jnp.float32)
-    thin = jnp.zeros((1, PIECE), jnp.float32)
-    for k, ref in enumerate((fpos_ref, fvel_ref)):
-        value = jnp.concatenate([jnp.concatenate([ref[...], thin], axis=0), wide], axis=1)
-        zown[4 * k : 4 * k + 4, :] = pltpu.roll(jnp.concatenate([value, value], axis=0), col * PIECE, 1)[0:4]
-    pl.semaphore_wait(barrier, len(partners))
-    for t in range(COLS - 1, 0, -1):
-        remote(zown, zrecv.at[col], z_send, z_recv, (row, line(t))).start()
     for d in range(8):
         halo_copy(0, d).start()
-    zrecv[col] = zown[...]
+    for t in (2, 1, 3):
+        remote(vsend, vrecv.at[pz], v_send, v_recv, line(t)).start()
     for load in loads[4:]:
         load.wait()
+    raw = [charge_raw[pl.ds(h, ROWS, stride=2), :] for h in range(2)]
+    charges = ordered(jnp.concatenate(raw, axis=1))
     for h in range(2):
-        charge_ref[:, 128 * h : 128 * h + 128] = charge_raw[pl.ds(h, ROWS, stride=2), :]
-    own_charge = charge_ref[pl.ds(row, 1), :]
+        charge_ref[h] = charges[:, 128 * h : 128 * h + 128]
+    own_charge = charge_ref[pk, pl.ds(row, 1), :]
     owner = owner_line()
-    corner[0:1, :] = lax.shift_right_logical(owner, 6).astype(jnp.float32)
-    corner[1:2, :] = (owner & 63).astype(jnp.float32)
-    index = lax.broadcasted_iota(jnp.int32, (ROWS, MOL), 0) * MOL + lax.broadcasted_iota(jnp.int32, (ROWS, MOL), 1)
-    banned = excl_ref[...]
-    hit = jnp.broadcast_to(banned[0:1, :], (ROWS, MOL)) == index
+    for h in range(2):
+        corner[0, h] = lax.shift_right_logical(owner[:, 128 * h : 128 * h + 128], 6).astype(jnp.float32)
+        corner[1, h] = (owner[:, 128 * h : 128 * h + 128] & 63).astype(jnp.float32)
+    member = lax.broadcasted_iota(jnp.int32, (ROWS, 128), 0)
+    other = 1 - pk
+    banned = lax.shift_right_logical(ordered(jnp.concatenate([excl_ref[...], excl_ref[...]], axis=0)), 8)
+    banned = banned[:, 0:128] * other + banned[:, 128:256] * pk
+    hit = jnp.broadcast_to(banned[0:1, :], (ROWS, 128)) == member
     for e in range(1, 4):
-        hit = hit | (jnp.broadcast_to(banned[e : e + 1, :], (ROWS, MOL)) == index)
-    barred[...] = jnp.where(hit, charge_ref[...], 0.0)
+        hit = hit | (jnp.broadcast_to(banned[e : e + 1, :], (ROWS, 128)) == member)
+    barred[...] = jnp.where(hit, charge_ref[pk], 0.0)
     fill_table(spos_ref)
     slow_start(spos_ref)
-
-    whole = zrecv.at[0 : COLS - 1]
-    remote(whole, whole, z_send, z_recv, (row, line(1))).wait_recv()
-    both = zrecv[0]
-    for c in range(1, COLS):
-        both = both + zrecv[c]
-    pos, vel = both[0:4], both[4:8]
-
-    gather_start(0, pos)
     for d in range(8):
         halo_copy(0, d).wait_recv()
-    slow_pairs(0, 0, 18)
-    arrivals(0, 1, ROWS)
-    env_rows(0)
+    slow_pairs(0, 0, 8)
+
+    whole = precv.at[0 : ROWS * COLS - 1]
+    remote(whole, whole, p_send, p_recv, line(1)).wait_recv()
+    lane = lax.shift_right_logical(lax.broadcasted_iota(jnp.int32, (ROWS, 128), 1), 5)
+    for k in range(2):
+        blocks = [precv[(k * 4 + z) * ROWS : (k * 4 + z) * ROWS + ROWS, 0, :] for z in range(4)]
+        for comp in range(3):
+            out = None
+            for z in range(4):
+                shift = (32 * (z - comp)) % 128
+                part = pltpu.roll(blocks[z], shift, 1) if shift else blocks[z]
+                out = part if out is None else jnp.where(lane == z, part, out)
+            mat[comp, k] = out
+    env_rows()
+    zero_line = jnp.zeros((1, 128), jnp.float32)
+    pos = jnp.concatenate([mat[comp, pk, pl.ds(row, 1), :] for comp in range(3)] + [zero_line], axis=0)
+    own_columns(pos)
     fast_rows(0, 0, ROWS, False)
     force = fast_end(pos)
-    slow_pairs(0, 18, 22)
-    env_middle(0)
-    slow_pairs(0, 22, 32)
-    slow_end()
+    whole = vrecv.at[0 : LINE - 1]
+    remote(whole, whole, v_send, v_recv, line(1)).wait_recv()
+    rows = []
+    lane = lax.shift_right_logical(lax.broadcasted_iota(jnp.int32, (8, 128), 1), 5)
     for comp in range(3):
-        v = svel_ref[comp] + half_outer * ((slow_coupling * scharge_ref[...]) * sforce[comp])
-        svel_out[comp] = v
-        spos_out[comp] = spos_ref[comp] + outer_dt * v
-    fill_halo(1, spos_out)
-    for d in range(8):
-        halo_copy(1, d).start()
-    vel = vel + half_outer * env_end(0)
+        out = None
+        for z in range(LINE):
+            shift = (32 * (z - comp)) % 128
+            part = jnp.broadcast_to(vrecv[z], (8, 128))
+            part = pltpu.roll(part, shift, 1) if shift else part
+            out = part if out is None else jnp.where(lane == z, part, out)
+        rows.append(out[0:1])
+    vel = jnp.concatenate(rows + [zero_line], axis=0)
+    slow_pairs(0, 8, 18)
+    env_middle()
+    slow_pairs(0, 18, 28)
+    vel = vel + half_outer * env_end()
     for g in range(1, INNER + 1):
         vel = vel + (0.5 * inner_dt) * force
         pos = pos + inner_dt * vel
         gather_start(g, pos)
         if g == 1:
-            fill_table(spos_out)
+            slow_pairs(0, 28, 32)
+            slow_end()
+            for comp in range(3):
+                v = svel_ref[comp] + half_outer * ((slow_coupling * scharge_ref[...]) * sforce[comp])
+                svel_out[comp] = v
+                spos_out[comp] = spos_ref[comp] + outer_dt * v
+            fill_halo(1, spos_out)
+            for d in range(8):
+                halo_copy(1, d).start()
             slow_start(spos_out)
         elif g == 2:
             for d in range(8):
                 halo_copy(1, d).wait_recv()
-            slow_pairs(1, 0, 6)
+            slow_pairs(1, 0, 10)
         elif g == 3:
-            slow_pairs(1, 6, 12)
+            slow_pairs(1, 10, 20)
         else:
-            slow_pairs(1, 12, 18)
+            fill_table(spos_out)
+            slow_pairs(1, 20, 24)
+        arrive_core(g)
         fast_rows(g, 0, 1, False)
         if g < INNER:
             fast_rows(g, 1, ROWS, True)
@@ -434,38 +500,39 @@
             fast_rows(g, 12, ROWS, False)
             force = fast_end(pos)
             vel = vel + (0.5 * inner_dt) * force
-    slow_pairs(1, 18, 32)
+    slow_pairs(1, 24, 32)
     slow_end()
     for comp in range(3):
         svel_out[comp] = svel_out[comp] + half_outer * ((slow_coupling * scharge_ref[...]) * sforce[comp])
-    back = lax.rem(MOL - col * PIECE, MOL)
+    back = lax.rem(128 - pz * PIECE, 128)
 
     def own_lanes(value):
         return pltpu.roll(jnp.concatenate([value, value], axis=0), back, 1)
 
     fpos_out[...] = own_lanes(pos)[0:3, 0:PIECE]
     vel = own_lanes(vel)
-    scale = (half_outer * slow_coupling) * own_lanes(jnp.broadcast_to(own_charge, (4, MOL)))[0:1, 0:PIECE]
+    scale = (half_outer * slow_coupling) * own_lanes(jnp.broadcast_to(own_charge, (4, 128)))[0:1, 0:PIECE]
     total = env_total()
     for comp in range(3):
         part = pltpu.roll(jnp.broadcast_to(total, (8, 128)), 128 - 32 * comp, 1) if comp else total
         fvel_out[comp : comp + 1, :] = vel[comp : comp + 1, 0:PIECE] + scale * part[0:1, 0:PIECE]
 
-    whole = zrecv.at[0 : COLS - 1]
-    remote(whole, whole, z_send, z_recv, (row, line(1))).wait_send()
     for buf in range(2):
         for d in range(8):
             halo_copy(buf, d).wait_send()
-    for ref, count, send, recv in (
-        (erecv.at[0], ROWS, e_send.at[0], e_recv.at[0]),
-        (zrecv2.at[0], COLS, y_send.at[0], y_recv.at[0]),
+    sent = [
+        (precv, ROWS * COLS, p_send, p_recv),
+        (vrecv, LINE, v_send, v_recv),
+        (erecv, 2 * ROWS, e_send, e_recv),
+        (zrecv2, LINE, y_send, y_recv),
         (drecv, ROWS * COLS, d_send, d_recv),
-    ):
+    ]
+    for ref, count, send, recv in sent:
         whole = ref.at[0 : count - 1]
-        remote(whole, whole, send, recv, (row, line(1))).wait_send()
-    for g in range(INNER + 1):
-        whole = gath.at[g, 0 : ROWS - 1]
-        remote(whole, whole, g_send.at[g], g_recv.at[g, 0], (row, line(1))).wait_send()
+        remote(whole, whole, send, recv, line(1)).wait_send()
+    for g in range(1, INNER + 1):
+        whole = erecv.at[0 : 2 * ROWS - 1]
+        remote(whole, whole, g_send.at[g], g_recv.at[g, 0], line(1)).wait_send()
 
 
 def finish(*refs):
@@ -501,17 +568,20 @@
             pltpu.VMEM((3, CELLS, CELL), f32),
             pltpu.VMEM((CELLS, CELL), f32),
             pltpu.SMEM((NBR, CR, CC), jnp.int32),
-            pltpu.VMEM((ROWS, MOL), f32),
+            pltpu.VMEM((2, ROWS, 128), f32),
             dma((9,)),
-            pltpu.VMEM((COLS, 8, MOL), f32),
-            pltpu.VMEM((INNER + 1, ROWS, 4, MOL), f32),
-            pltpu.VMEM((3, ROWS, MOL), f32),
-            pltpu.VMEM((2, ROWS, 4, MOL), f32),
-            pltpu.VMEM((2, ROWS, 4, MOL), f32),
-            pltpu.VMEM((2, 4, MOL), f32),
-            pltpu.VMEM((2, COLS, 4, MOL), f32),
-            pltpu.VMEM((3, MOL, 128), f32),
-            pltpu.VMEM((3, MOL, 128), f32),
+            pltpu.VMEM((1, 128), f32),
+            pltpu.VMEM((ROWS * COLS, 1, 128), f32),
+            pltpu.VMEM((1, 128), f32),
+            pltpu.VMEM((LINE, 1, 128), f32),
+            pltpu.VMEM((INNER + 1, ROWS, 2, 4, 128), f32),
+            pltpu.VMEM((3, 2, ROWS, 128), f32),
+            pltpu.VMEM((ROWS, 2, 4, 128), f32),
+            pltpu.VMEM((2 * ROWS, 4, 128), f32),
+            pltpu.VMEM((4, 128), f32),
+            pltpu.VMEM((LINE, 4, 128), f32),
+            pltpu.VMEM((3, 128, 128), f32),
+            pltpu.VMEM((3, 128, 128), f32),
             pltpu.VMEM((CR + 4, CC + 4, 4, CELL), f32),
             pltpu.VMEM((CR + 4, CC + 4, 4, CELL), f32),
             pltpu.VMEM((3, CELL, CELL), f32),
@@ -520,19 +590,20 @@
             pltpu.VMEM((3, CELL, CELL), f32),
             pltpu.VMEM((3, CELLS, CELL), f32),
             pltpu.VMEM((4 * CELL, MOL), f32),
-            pltpu.VMEM((8, MOL), f32),
             pltpu.VMEM((ROWS * COLS, 1, 128), f32),
             pltpu.VMEM((ROWS * COLS, 1, 128), f32),
-            pltpu.VMEM((2, MOL), f32),
-            pltpu.VMEM((ROWS, MOL), f32),
+            pltpu.VMEM((2, 2, 1, 128), f32),
+            pltpu.VMEM((ROWS, 128), f32),
+            dma,
+            dma,
             dma,
             dma,
             dma((INNER + 1,)),
             dma((INNER + 1, ROWS)),
-            dma((2,)),
-            dma((2,)),
-            dma((2,)),
-            dma((2,)),
+            dma,
+            dma,
+            dma,
+            dma,
             dma((2, 8)),
             dma((2, 8)),
             dma,

time: 65.7 us -> 61.7 us (0.939)
  Pallas kernels: 64.3 us -> 60.2 us
    pallas_call x1, Pallas kernels: 62.9 us -> 58.7 us  [per_device(): pl.pallas_call(kernel, out_shape=(jax.ShapeDtypeStruct((3, PIECE), f32),...]
where the time goes in v3:
time: 61.7 us; the launch traced here: 60.8 us
  Pallas kernels  60.2 us (98%)
  between operations  0.64 us (1%)
    pallas_call x1, Pallas kernels, per_device(): pl.pallas_call(kernel, out_shape=(jax.ShapeDtypeStruct((3, PIECE), f32),...  58.7 us
    pallas_call x1, Pallas kernels, per_device(): pl.pallas_call(finish, out_shape=[jax.ShapeDtypeStruct(o.shape, f32) for...  1.48 us

profile of v3, /device:TPU:0, one launch (start us, length us, event | category | flops | bytes accessed | tf_op | source)
XLA Modules:
  0.0 60.8 jit_solution(11493632153068814625)
XLA Ops:
  0.6 58.7 %shard_map.120 = (f32[3,32]{1,0:T(4,128)}, f32[3,32]{1,0:T(4,128)}, f32[3,32,128]{2,1,0:T(8,128)}, f32[3,32,128]{2,1,0:T(8,128)}) custom-call(f32[3,32]{1,0:T(4,128)} %fpos_in.1, f32[3,32]{1,0:T(4,128)} %fvel_in.1, f32[32,128]{1,0:T(8,128)} %bitcast.12, s32[32,128]{1,0:T(8,128)} %bitcast.13, s32[4,4096]{1,0:T(4,128)} %bitcast.9, f32[3,32,128]{2,1,0:T(8,128)} %bitcast.10, ...), custom_call_target="tpu_custom_call" | custom-call | tf_op jit(solution)/shard_map/pallas_call | solution.py:551
  59.3 1.5 %shard_map.121 = (f32[3,32]{1,0:T(4,128)}, f32[3,32]{1,0:T(4,128)}, f32[3,32,128]{2,1,0:T(8,128)}, f32[3,32,128]{2,1,0:T(8,128)}) custom-call(f32[3,32]{1,0:T(4,128)} %get-tuple-element.12.refs_0_, f32[3,32]{1,0:T(4,128)} %get-tuple-element.13.refs_1_, f32[3,32,128]{2,1,0:T(8,128)} %get-tuple-element.14.refs_2_, f32[3,32,128]{2,1,0:T(8,128)} %get-tuple-element.15.refs_3_), custom_call_target="tpu_custom_call" | custom-call | tf_op jit(solution)/shard_map/pallas_call | solution.py:626

commit v4 on v3

--- a/solution.py
+++ b/solution.py
@@ -38,13 +38,15 @@
     fpos_in, fvel_in, charge_in, owner_in, excl_in, spos_in, svel_in, scharge_in, nbr_in,
     fpos_out, fvel_out, spos_out, svel_out,
     fpos_ref, fvel_ref, charge_raw, owner_ref, excl_ref, spos_ref, svel_ref, scharge_ref, nbr_ref, charge_ref, in_sem,
-    psend, precv, vsend, vrecv, gath, mat, esend, erecv, zsend2, zrecv2, acol, facc, halo_0, halo_1, scol_0, scol_1, sacc_0, sacc_1, sforce, table, dsend, drecv, corner, barred,
+    psend, precv, vsend, vrecv, gath, mat, esend, erecv, zsend2, zrecv2, acol, facc, halo_0, halo_1, scol_0, scol_1, sacc_0, sacc_1, sforce, table, eforce, dsend, drecv, corner, barred,
     p_send, p_recv, v_send, v_recv, g_send, g_recv, e_send, e_recv, y_send, y_recv, h_send, h_recv, d_send, d_recv,
 ):
     row = lax.axis_index("row")
     col = lax.axis_index("col")
     halos = (halo_0, halo_1)
     px, py, pz, pk = lax.div(row, 4), lax.rem(row, 4), lax.div(col, 2), lax.rem(col, 2)
+
+    near = lax.div(px, 2)
 
     def peer(t):
         if isinstance(t, int):
@@ -226,15 +228,16 @@
                 jnp.transpose(data), pick, precision=lax.Precision.HIGHEST, preferred_element_type=jnp.float32
             )
 
-    def env_partial():
-        mx, my, mz = (jnp.concatenate([mat[comp, 0], mat[comp, 1]], axis=1) for comp in range(3))
+    def env_half(part):
+        rows8 = pl.ds(pl.multiple_of(part * 8, 8), 8)
+        mx, my, mz = (jnp.concatenate([mat[comp, h, rows8, :] for h in range(2)], axis=1) for comp in range(3))
 
         def body(jb, carry):
             fx, fy, fz = carry
-            for k in range(4):
-                j = jb * 4 + k
+            for n in range(8):
+                j = jb * 8 + n
                 ox, oy, oz, oq = (
-                    jnp.broadcast_to(table[pl.ds(comp * CELL + j, 1), :], (ROWS, MOL)) for comp in range(4)
+                    jnp.broadcast_to(table[pl.ds(comp * CELL + j, 1), :], (8, MOL)) for comp in range(4)
                 )
                 dx, dy, dz = mx - ox, my - oy, mz - oz
                 s = (dx * dx + dy * dy) + (dz * dz + 0.5)
@@ -243,28 +246,28 @@
                 fx, fy, fz = fx + w * dx, fy + w * dy, fz + w * dz
             return fx, fy, fz
 
-        zero = jnp.zeros((ROWS, MOL), jnp.float32)
-        return lax.fori_loop(0, CELL // 4, body, (zero, zero, zero))
+        zero = jnp.zeros((8, MOL), jnp.float32)
+        force = lax.fori_loop(0, CELL // 8, body, (zero, zero, zero))
+        for comp in range(3):
+            eforce[comp, rows8, :] = force[comp]
 
     def env_rows():
-        force = env_partial()
         for r in range(ROWS):
             for k in range(2):
                 for comp in range(3):
-                    esend[r, k, comp : comp + 1, :] = force[comp][r : r + 1, 128 * k : 128 * k + 128]
+                    esend[r, k, comp : comp + 1, :] = eforce[comp, r : r + 1, 128 * k : 128 * k + 128]
                 esend[r, k, 3:4, :] = jnp.zeros((1, 128), jnp.float32)
         for to, r, k in plane():
             remote(esend.at[r, k], erecv.at[row * 2 + pk], e_send, e_recv, to).start()
         erecv[row * 2 + pk] = esend[row, pk]
 
     def env_direct():
-        force = env_partial()
         lane = lax.broadcasted_iota(jnp.int32, (ROWS, 128), 1)
         for c in range(COLS):
             h, j = c // 4, c % 4
             line_ = jnp.zeros((ROWS, 128), jnp.float32)
             for comp in range(3):
-                part = force[comp][:, 128 * h : 128 * h + 128]
+                part = eforce[comp, :, 128 * h : 128 * h + 128]
                 shift = (32 * (comp - j)) % 128
                 part = pltpu.roll(part, shift, 1) if shift else part
                 line_ = jnp.where(lax.shift_right_logical(lane, 5) == comp, part, line_)
@@ -309,8 +312,7 @@
             acol[comp] = column(line_)
         facc[...] = jnp.zeros_like(facc)
 
-    def arrive(g, t):
-        r = peer(t)
+    def arrive(g, r):
         slot = gath.at[g, r]
         remote(slot, slot, g_send.at[g], g_recv.at[g, r], line(1)).wait_recv()
         for k in range(2):
@@ -323,8 +325,7 @@
         for comp in range(3):
             mat[comp, 1 - pk, pl.ds(row, 1), :] = gath[g, row, 1 - pk, comp : comp + 1, :]
 
-    def fast_row(g, t):
-        r = peer(t)
+    def fast_row(r):
         halves = [
             (
                 mat[0, h, pl.ds(r, 1), :] + corner[0, h],
@@ -352,21 +353,25 @@
             facc[1, 8 * i : 8 * i + 8, :] = fy
             facc[2, 8 * i : 8 * i + 8, :] = fz
 
-    def fast_rows(g, t0, t1, waiting):
+    def fast_rows(g, count, which, waiting=True, computing=True):
         def body(t, carry):
+            r = which(t)
             if waiting:
-                arrive(g, t)
-            fast_row(g, t)
+                arrive(g, r)
+            if computing:
+                fast_row(r)
             return carry
 
-        lax.fori_loop(t0, t1, body, 0)
-
-    def arrivals(g, t0, t1):
-        def body(t, carry):
-            arrive(g, t)
-            return carry
-
-        lax.fori_loop(t0, t1, body, 0)
+        lax.fori_loop(0, count, body, 0)
+
+    def same_x(t):
+        return px * 4 + lax.rem(py + 1 + t, 4)
+
+    def next_x(t):
+        return (px + 1 - 2 * lax.rem(px, 2)) * 4 + lax.rem(py + t, 4)
+
+    def far_x(t):
+        return (1 - near) * 8 + t
 
     def fast_end(pos):
         d = [jnp.broadcast_to(pos[comp : comp + 1, :], (ROWS, 128)) - mat[comp, pk] for comp in range(3)]
@@ -395,7 +400,7 @@
     vrecv[pz] = vsend[...]
     pl.semaphore_wait(barrier, ROWS * COLS - 1)
     for to, _ in everyone():
-        remote(psend, precv.at[mine], p_send, p_recv, to).start()
+        remote(psend, precv.at[mine], p_send, p_recv.at[near], to).start()
     loads[0].wait()
     loads[1].wait()
     fill_halo(0, spos_ref)
@@ -424,27 +429,26 @@
     barred[...] = jnp.where(hit, charge_ref[pk], 0.0)
     fill_table(spos_ref)
     slow_start(spos_ref)
-    for d in range(8):
-        halo_copy(0, d).wait_recv()
-    slow_pairs(0, 0, 8)
-
-    whole = precv.at[0 : ROWS * COLS - 1]
-    remote(whole, whole, p_send, p_recv, line(1)).wait_recv()
-    lane = lax.shift_right_logical(lax.broadcasted_iota(jnp.int32, (ROWS, 128), 1), 5)
-    for k in range(2):
-        blocks = [precv[(k * 4 + z) * ROWS : (k * 4 + z) * ROWS + ROWS, 0, :] for z in range(4)]
-        for comp in range(3):
-            out = None
-            for z in range(4):
-                shift = (32 * (z - comp)) % 128
-                part = pltpu.roll(blocks[z], shift, 1) if shift else blocks[z]
-                out = part if out is None else jnp.where(lane == z, part, out)
-            mat[comp, k] = out
+
+    lane = lax.shift_right_logical(lax.broadcasted_iota(jnp.int32, (8, 128), 1), 5)
+    for part in (near, 1 - near):
+        whole = precv.at[0 : 63 if part is near else 64]
+        remote(whole, whole, p_send, p_recv.at[part], line(1)).wait_recv()
+        for k in range(2):
+            blocks = [precv[pl.ds((k * 4 + z) * ROWS + part * 8, 8), 0, :] for z in range(4)]
+            for comp in range(3):
+                out = None
+                for z in range(4):
+                    shift = (32 * (z - comp)) % 128
+                    block = pltpu.roll(blocks[z], shift, 1) if shift else blocks[z]
+                    out = block if out is None else jnp.where(lane == z, block, out)
+                mat[comp, k, pl.ds(pl.multiple_of(part * 8, 8), 8), :] = out
+        env_half(part)
     env_rows()
     zero_line = jnp.zeros((1, 128), jnp.float32)
     pos = jnp.concatenate([mat[comp, pk, pl.ds(row, 1), :] for comp in range(3)] + [zero_line], axis=0)
     own_columns(pos)
-    fast_rows(0, 0, ROWS, False)
+    fast_rows(0, ROWS, lambda t: t, waiting=False)
     force = fast_end(pos)
     whole = vrecv.at[0 : LINE - 1]
     remote(whole, whole, v_send, v_recv, line(1)).wait_recv()
@@ -459,16 +463,20 @@
             out = part if out is None else jnp.where(lane == z, part, out)
         rows.append(out[0:1])
     vel = jnp.concatenate(rows + [zero_line], axis=0)
+    for d in range(8):
+        halo_copy(0, d).wait_recv()
+    slow_pairs(0, 0, 8)
+    env_middle()
     slow_pairs(0, 8, 18)
-    env_middle()
-    slow_pairs(0, 18, 28)
     vel = vel + half_outer * env_end()
     for g in range(1, INNER + 1):
         vel = vel + (0.5 * inner_dt) * force
         pos = pos + inner_dt * vel
         gather_start(g, pos)
         if g == 1:
-            slow_pairs(0, 28, 32)
+            slow_pairs(0, 18, 26)
+        elif g == 2:
+            slow_pairs(0, 26, 32)
             slow_end()
             for comp in range(3):
                 v = svel_ref[comp] + half_outer * ((slow_coupling * scharge_ref[...]) * sforce[comp])
@@ -478,29 +486,33 @@
             for d in range(8):
                 halo_copy(1, d).start()
             slow_start(spos_out)
-        elif g == 2:
+        elif g == 3:
+            arrive_core(g)
+            fast_row(row)
             for d in range(8):
                 halo_copy(1, d).wait_recv()
-            slow_pairs(1, 0, 10)
-        elif g == 3:
-            slow_pairs(1, 10, 20)
+            slow_pairs(1, 0, 8)
         else:
             fill_table(spos_out)
-            slow_pairs(1, 20, 24)
-        arrive_core(g)
-        fast_rows(g, 0, 1, False)
+            slow_pairs(1, 8, 14)
+        if g != 3:
+            arrive_core(g)
+            fast_row(row)
         if g < INNER:
-            fast_rows(g, 1, ROWS, True)
-            force = fast_end(pos)
-            vel = vel + (0.5 * inner_dt) * force
+            fast_rows(g, ROWS - 1, lambda t: peer(t + 1))
         else:
-            fast_rows(g, 1, 12, True)
-            arrivals(g, 12, ROWS)
+            fast_rows(g, 3, same_x)
+            fast_rows(g, 2, next_x)
+            fast_rows(g, 2, lambda t: next_x(t + 2), computing=False)
+            env_half(near)
+            fast_rows(g, 8, far_x, computing=False)
+            env_half(1 - near)
             env_direct()
-            fast_rows(g, 12, ROWS, False)
-            force = fast_end(pos)
-            vel = vel + (0.5 * inner_dt) * force
-    slow_pairs(1, 24, 32)
+            fast_rows(g, 2, lambda t: next_x(t + 2), waiting=False)
+            fast_rows(g, 8, far_x, waiting=False)
+        force = fast_end(pos)
+        vel = vel + (0.5 * inner_dt) * force
+    slow_pairs(1, 14, 32)
     slow_end()
     for comp in range(3):
         svel_out[comp] = svel_out[comp] + half_outer * ((slow_coupling * scharge_ref[...]) * sforce[comp])
@@ -521,7 +533,7 @@
         for d in range(8):
             halo_copy(buf, d).wait_send()
     sent = [
-        (precv, ROWS * COLS, p_send, p_recv),
+        (precv, ROWS * COLS, p_send, p_recv.at[0]),
         (vrecv, LINE, v_send, v_recv),
         (erecv, 2 * ROWS, e_send, e_recv),
         (zrecv2, LINE, y_send, y_recv),
@@ -590,12 +602,13 @@
             pltpu.VMEM((3, CELL, CELL), f32),
             pltpu.VMEM((3, CELLS, CELL), f32),
             pltpu.VMEM((4 * CELL, MOL), f32),
+            pltpu.VMEM((3, ROWS, MOL), f32),
             pltpu.VMEM((ROWS * COLS, 1, 128), f32),
             pltpu.VMEM((ROWS * COLS, 1, 128), f32),
             pltpu.VMEM((2, 2, 1, 128), f32),
             pltpu.VMEM((ROWS, 128), f32),
             dma,
-            dma,
+            dma((2,)),
             dma,
             dma,
             dma((INNER + 1,)),

time: 61.7 us -> 59.7 us (0.968)
  Pallas kernels: 60.2 us -> 57.9 us
    pallas_call x1, Pallas kernels: 58.7 us -> 56.4 us  [per_device(): pl.pallas_call(kernel, out_shape=(jax.ShapeDtypeStruct((3, PIECE), f32),...]
where the time goes in v4:
time: 59.7 us; the launch traced here: 58.5 us
  Pallas kernels  57.9 us (97%)
  between operations  0.64 us (1%)
    pallas_call x1, Pallas kernels, per_device(): pl.pallas_call(kernel, out_shape=(jax.ShapeDtypeStruct((3, PIECE), f32),...  56.4 us
    pallas_call x1, Pallas kernels, per_device(): pl.pallas_call(finish, out_shape=[jax.ShapeDtypeStruct(o.shape, f32) for...  1.48 us

profile of v4, /device:TPU:0, one launch (start us, length us, event | category | flops | bytes accessed | tf_op | source)
XLA Modules:
  0.0 58.5 jit_solution(1653568114285990214)
XLA Ops:
  0.6 56.4 %shard_map.120 = (f32[3,32]{1,0:T(4,128)}, f32[3,32]{1,0:T(4,128)}, f32[3,32,128]{2,1,0:T(8,128)}, f32[3,32,128]{2,1,0:T(8,128)}) custom-call(f32[3,32]{1,0:T(4,128)} %fpos_in.1, f32[3,32]{1,0:T(4,128)} %fvel_in.1, f32[32,128]{1,0:T(8,128)} %bitcast.12, s32[32,128]{1,0:T(8,128)} %bitcast.13, s32[4,4096]{1,0:T(4,128)} %bitcast.9, f32[3,32,128]{2,1,0:T(8,128)} %bitcast.10, ...), custom_call_target="tpu_custom_call" | custom-call | tf_op jit(solution)/shard_map/pallas_call | solution.py:563
  57.1 1.5 %shard_map.121 = (f32[3,32]{1,0:T(4,128)}, f32[3,32]{1,0:T(4,128)}, f32[3,32,128]{2,1,0:T(8,128)}, f32[3,32,128]{2,1,0:T(8,128)}) custom-call(f32[3,32]{1,0:T(4,128)} %get-tuple-element.12.refs_0_, f32[3,32]{1,0:T(4,128)} %get-tuple-element.13.refs_1_, f32[3,32,128]{2,1,0:T(8,128)} %get-tuple-element.14.refs_2_, f32[3,32,128]{2,1,0:T(8,128)} %get-tuple-element.15.refs_3_), custom_call_target="tpu_custom_call" | custom-call | tf_op jit(solution)/shard_map/pallas_call | solution.py:639
